TPU v7x, 8 devices: a whole 2x2x1 slice. The times are simulated.
8 devices in a mesh: dp: 1 (over z), cy: 2 (over y), cx: 4 (over x, core).
Axes of the slice: x: 2, y: 2, z: 1, core: 2. Of those that a mesh axis runs over, the one named last changes fastest.
Arguments:
- queries: bfloat16 [16384, 12, 128], P(('dp', 'cx', 'cy'))
- keys: bfloat16 [16384, 2, 128], P(('dp', 'cx', 'cy'))
- values: bfloat16 [16384, 2, 128], P(('dp', 'cx', 'cy'))
- doc_ids: int32 [16384], P(('dp', 'cx', 'cy'))
Outputs:
- output: bfloat16 [16384, 12, 128], P(('dp', 'cx', 'cy'))
All inputs are finite; a program needn't handle non-finite values.
Results may differ from a plain program's by a relative error of at most 0.00125057.
Values are sent between devices in bfloat16 or wider.
A program may use at most 1 GiB of HBM per device.

v0:
```python
import jax
import jax.numpy as jnp
from jax import lax
from jax.sharding import PartitionSpec as P

NEG_BIG = -1e30


def piece_update(run_stats, q_piece, k_piece, v_piece, allowed):
    max_old, sum_old, acc_old = run_stats
    score_scale = q_piece.shape[-1] ** -0.5
    scores = jnp.einsum('qgjd,kgd->gqjk', q_piece, k_piece, preferred_element_type=jnp.float32) * score_scale
    key_mask = allowed[None, :, None, :]
    max_new = jnp.maximum(max_old, jnp.max(jnp.where(key_mask, scores, NEG_BIG), axis=-1))
    weights = jnp.exp(jnp.where(key_mask, scores - max_new[..., None], NEG_BIG))
    rescale = jnp.exp(max_old - max_new)
    sum_new = sum_old * rescale + jnp.sum(weights, axis=-1)
    acc_new = acc_old * rescale[..., None] + jnp.einsum('gqjk,kgd->gqjd', weights.astype(jnp.bfloat16), v_piece, preferred_element_type=jnp.float32)
    return max_new, sum_new, acc_new


def keep_stats(run_stats, q_piece, k_piece, v_piece, allowed):
    return run_stats


def block_update(run_stats, q_pieces, q_pos, q_docs, k_block, v_block, doc_block, source, group_size):
    piece_len = k_block.shape[0] // 2
    offsets = jnp.arange(piece_len)
    k_piece_ids = (source, 2 * group_size - 1 - source)
    new_stats = []
    for q_idx in range(2):
        cur_stats = run_stats[q_idx]
        for k_idx in range(2):
            row_lo = k_idx * piece_len
            k_pos = k_piece_ids[k_idx] * piece_len + offsets
            k_docs = doc_block[row_lo:row_lo + piece_len]
            allowed = (k_pos[None, :] <= q_pos[q_idx][:, None]) & (k_docs[None, :] == q_docs[q_idx][:, None])
            cur_stats = lax.cond(jnp.any(allowed), piece_update, keep_stats, cur_stats, q_pieces[q_idx], k_block[row_lo:row_lo + piece_len], v_block[row_lo:row_lo + piece_len], allowed)
        new_stats.append(cur_stats)
    return tuple(new_stats)


def solution(mesh):
    size_cx = mesh.shape['cx']
    size_cy = mesh.shape['cy']
    group_size = size_cx * size_cy
    cy_perm = [(member, (member + 1) % size_cy) for member in range(size_cy)]
    cx_perm = [(member, (member + 1) % size_cx) for member in range(size_cx)]
    seq_spec = P(('dp', 'cx', 'cy'), None, None)
    doc_spec = P(('dp', 'cx', 'cy'))

    def per_device(q_loc, k_loc, v_loc, doc_loc):
        tok_dev, num_heads, head_dim = q_loc.shape
        kv_heads = k_loc.shape[1]
        q_per_kv = num_heads // kv_heads
        piece_len = tok_dev // 2
        idx_x = lax.axis_index('cx')
        idx_y = lax.axis_index('cy')
        my_rank = idx_x * size_cy + idx_y
        offsets = jnp.arange(piece_len)
        q_pieces = q_loc.reshape(2, piece_len, kv_heads, q_per_kv, head_dim)
        q_pos = (my_rank * piece_len + offsets, (2 * group_size - 1 - my_rank) * piece_len + offsets)
        q_docs = (doc_loc[:piece_len], doc_loc[piece_len:])
        stat_shape = (kv_heads, piece_len, q_per_kv)
        fresh = (jnp.full(stat_shape, NEG_BIG, jnp.float32), jnp.zeros(stat_shape, jnp.float32), jnp.zeros(stat_shape + (head_dim,), jnp.float32))

        def visit(run_stats, block_in, outer_step, inner_step):
            source = ((idx_x - outer_step) % size_cx) * size_cy + (idx_y - inner_step) % size_cy
            return block_update(run_stats, q_pieces, q_pos, q_docs, block_in[0], block_in[1], block_in[2], source, group_size)

        def row_pass(outer_step, row_block, run_stats):
            def inner_body(inner_step, carry):
                cur_block, cur_stats = carry
                cur_stats = visit(cur_stats, cur_block, outer_step, inner_step)
                cur_block = tuple(lax.ppermute(block_arr, 'cy', cy_perm) for block_arr in cur_block)
                return cur_block, cur_stats
            last_block, run_stats = lax.fori_loop(0, size_cy - 1, inner_body, (row_block, run_stats))
            return visit(run_stats, last_block, outer_step, size_cy - 1)

        def outer_body(outer_step, carry):
            row_block, cur_stats = carry
            cur_stats = row_pass(outer_step, row_block, cur_stats)
            row_block = tuple(lax.ppermute(block_arr, 'cx', cx_perm) for block_arr in row_block)
            return row_block, cur_stats

        last_row, run_stats = lax.fori_loop(0, size_cx - 1, outer_body, ((k_loc, v_loc, doc_loc), (fresh, fresh)))
        run_stats = row_pass(size_cx - 1, last_row, run_stats)
        normed = jnp.stack([stat_q[2] / stat_q[1][..., None] for stat_q in run_stats])
        return normed.astype(jnp.bfloat16).transpose(0, 2, 1, 3, 4).reshape(tok_dev, num_heads, head_dim)

    return jax.shard_map(per_device, mesh=mesh, in_specs=(seq_spec, seq_spec, seq_spec, doc_spec), out_specs=seq_spec, check_vma=False)
```

profile of v0, /device:TPU:7, one launch (start us, length us, event | category | flops | bytes accessed | tf_op | source)
XLA Modules:
  0.0 1483.7 jit_solution(18264459350985086585)
XLA Ops:
  21.1 1136.8 %while.115 = (s32[]{:T(128)}, bf16[2048,2,128]{2,0,1:T(8,128)(2,1)}, bf16[2048,2,128]{2,0,1:T(8,128)(2,1)}, s32[2048]{0:T(1024)}, f32[2,1024,6]{1,2,0:T(8,128)},...) while((s32[]{:T(128)}, bf16[2048,2,128]{2,0,1:T(8,128)(2,1)}, ...), condition=%wide.region_41.42_spmd.clone, body=%wide.region_0.41_spmd.clone.sunk | while | flops 52705828864 | bytes 1475274624 | solution.py:86
  38.6 32.0 %collective-permute-done.3 = s32[2048]{0:T(1024)S(1)} collective-permute-done((s32[2048]{0:T(1024)}, s32[2048]{0:T(1024)S(1)}, u32[]{:S(2)}, u32[]{:S(2)}) %collective-permute-start.3) | collective-permute-done | bytes 8224 | tf_op jit(solution)/shard_map/while/body/eval_jaxpr/while/body/eval_jaxpr/ppermute | solution.py:75
  88.1 67.1 %conditional.44 = ((f32[2,1024,6]{1,2,0:T(8,128)S(1)}, f32[2,1024,6]{1,2,0:T(8,128)S(1)}, f32[2,1024,6,128]{3,1,2,0:T(8,128)})) conditional(s32[]{:T(128)} %convert_element_type.264, (f32[2,1024,6]{1,2,0:T(8,128)S(1)}, f32[2,1024,6]{1,2,0:T(8,128)S(1)}, f32[2,1024,6,128]{3,1,2,0:T(8,128)}) %tuple.310, (pred[1024,1024]{0,1:T(8,128)(4,1)}, ...), branch_computations={%region_25.25_spmd, %region_26.0_spmd} | conditional | flops 6584033280 | bytes 177995872 | solution.py:38
  155.2 67.3 %conditional.45 = ((f32[2,1024,6]{1,2,0:T(8,128)S(1)}, f32[2,1024,6]{1,2,0:T(8,128)S(1)}, f32[2,1024,6,128]{3,1,2,0:T(8,128)})) conditional(s32[]{:T(128)} %convert_element_type.263, (f32[2,1024,6]{1,2,0:T(8,128)S(1)}, f32[2,1024,6]{1,2,0:T(8,128)S(1)}, f32[2,1024,6,128]{3,1,2,0:T(8,128)}) %get-tuple-element.1907, (pred[1024,1024]{0,1:T(8,128)(4,1)}, ...), branch_computations={%region_29.29_spmd, %region_30.32_spmd} | conditional | flops 6584033280 | bytes 177995872 | solution.py:38
  198.6 23.9 %multiply_add_fusion.10 = f32[2,1024,6,128]{3,1,2,0:T(8,128)} fusion(f32[2,1024,6,128]{3,1,2,0:T(8,128)} %get-tuple-element.1015, f32[2,1024,6]{1,2,0:T(8,128)S(1)} %get-tuple-element.1340, f32[2,1024,6,1024]{1,3,2,0:T(8,128)} %get-tuple-element.1404, f32[2,1024,6]{1,2,0:T(8,128)S(1)} %max.37, pred[1024,1024]{0,1:T(8,128)(4,1)S(1)} %copy-done.6, ...), kind=kOutput, calls=%fused_computation.78 | convolution fusion | flops 3274702848 | bytes 64585728 | tf_op jit(solution)/shard_map/while/body/eval_jaxpr/while/body/eval_jaxpr/cond/branch_1_fun/gqjk,kgd->gqjd/dot_general | solution.py:18
  222.6 67.0 %conditional.40 = ((f32[2,1024,6]{1,2,0:T(8,128)S(1)}, f32[2,1024,6]{1,2,0:T(8,128)S(1)}, f32[2,1024,6,128]{3,1,2,0:T(8,128)})) conditional(s32[]{:T(128)} %convert_element_type.260, (f32[2,1024,6]{1,2,0:T(8,128)S(1)}, f32[2,1024,6]{1,2,0:T(8,128)S(1)}, f32[2,1024,6,128]{3,1,2,0:T(8,128)}) %tuple.394, (pred[1024,1024]{0,1:T(8,128)(4,1)}, ...), branch_computations={%region_5.5_spmd, %region_6.8_spmd} | conditional | flops 6584033280 | bytes 177995872 | solution.py:38
  265.7 23.9 %multiply_add_fusion = f32[2,1024,6,128]{3,1,2,0:T(8,128)} fusion(f32[2,1024,6,128]{3,1,2,0:T(8,128)} %get-tuple-element.980, f32[2,1024,6]{1,2,0:T(8,128)S(1)} %get-tuple-element.1330, f32[2,1024,6,1024]{1,3,2,0:T(8,128)} %get-tuple-element.1394, f32[2,1024,6]{1,2,0:T(8,128)S(1)} %max.32, pred[1024,1024]{0,1:T(8,128)(4,1)S(1)} %copy-done.5, ...), kind=kOutput, calls=%fused_computation.8 | convolution fusion | flops 3274702848 | bytes 64585728 | tf_op jit(solution)/shard_map/while/body/eval_jaxpr/while/body/eval_jaxpr/cond/branch_1_fun/gqjk,kgd->gqjd/dot_general | solution.py:18
  294.4 69.3 %conditional.46 = ((f32[2,1024,6]{1,2,0:T(8,128)S(1)}, f32[2,1024,6]{1,2,0:T(8,128)S(1)}, f32[2,1024,6,128]{3,1,2,0:T(8,128)})) conditional(s32[]{:T(128)} %convert_element_type.262, (f32[2,1024,6]{1,2,0:T(8,128)S(1)}, f32[2,1024,6]{1,2,0:T(8,128)S(1)}, f32[2,1024,6,128]{3,1,2,0:T(8,128)}) %get-tuple-element.1908, (pred[1024,1024]{0,1:T(8,128)(4,1)}, ...), branch_computations={%region_33.33_spmd, %region_34.36_spmd} | conditional | flops 6584033280 | bytes 177995872 | solution.py:38
  339.7 23.9 %multiply_add_fusion.12 = f32[2,1024,6,128]{3,1,2,0:T(8,128)} fusion(f32[2,1024,6,128]{3,1,2,0:T(8,128)} %get-tuple-element.1022, f32[2,1024,6]{1,2,0:T(8,128)S(1)} %get-tuple-element.1342, f32[2,1024,6,1024]{1,3,2,0:T(8,128)} %get-tuple-element.1406, f32[2,1024,6]{1,2,0:T(8,128)S(1)} %max.38, pred[1024,1024]{0,1:T(8,128)(4,1)S(1)} %copy-done.3, ...), kind=kOutput, calls=%fused_computation.92 | convolution fusion | flops 3274702848 | bytes 64585728 | tf_op jit(solution)/shard_map/while/body/eval_jaxpr/cond/branch_1_fun/gqjk,kgd->gqjd/dot_general | solution.py:18
  364.1 73.3 %conditional.42 = ((f32[2,1024,6]{1,2,0:T(8,128)S(1)}, f32[2,1024,6]{1,2,0:T(8,128)S(1)}, f32[2,1024,6,128]{3,1,2,0:T(8,128)})) conditional(s32[]{:T(128)} %convert_element_type.258, (f32[2,1024,6]{1,2,0:T(8,128)S(1)}, f32[2,1024,6]{1,2,0:T(8,128)S(1)}, f32[2,1024,6,128]{3,1,2,0:T(8,128)}) %get-tuple-element.1904, (pred[1024,1024]{0,1:T(8,128)(4,1)}, ...), branch_computations={%region_13.13_spmd, %region_14.16_spmd} | conditional | flops 6584033280 | bytes 177995872 | solution.py:38
  413.4 23.9 %multiply_add_fusion.4 = f32[2,1024,6,128]{3,1,2,0:T(8,128)} fusion(f32[2,1024,6,128]{3,1,2,0:T(8,128)} %get-tuple-element.994, f32[2,1024,6]{1,2,0:T(8,128)S(1)} %get-tuple-element.1334, f32[2,1024,6,1024]{1,3,2,0:T(8,128)} %get-tuple-element.1398, f32[2,1024,6]{1,2,0:T(8,128)S(1)} %max.34, pred[1024,1024]{0,1:T(8,128)(4,1)S(1)} %copy-done.1, ...), kind=kOutput, calls=%fused_computation.36 | convolution fusion | flops 3274702848 | bytes 64585728 | tf_op jit(solution)/shard_map/while/body/eval_jaxpr/cond/branch_1_fun/gqjk,kgd->gqjd/dot_general | solution.py:18
  500.8 67.1 %conditional.44 = ((f32[2,1024,6]{1,2,0:T(8,128)S(1)}, f32[2,1024,6]{1,2,0:T(8,128)S(1)}, f32[2,1024,6,128]{3,1,2,0:T(8,128)})) conditional(s32[]{:T(128)} %convert_element_type.264, (f32[2,1024,6]{1,2,0:T(8,128)S(1)}, f32[2,1024,6]{1,2,0:T(8,128)S(1)}, f32[2,1024,6,128]{3,1,2,0:T(8,128)}) %tuple.310, (pred[1024,1024]{0,1:T(8,128)(4,1)}, ...), branch_computations={%region_25.25_spmd, %region_26.0_spmd} | conditional | flops 6584033280 | bytes 177995872 | solution.py:38
  568.8 72.7 %conditional.40 = ((f32[2,1024,6]{1,2,0:T(8,128)S(1)}, f32[2,1024,6]{1,2,0:T(8,128)S(1)}, f32[2,1024,6,128]{3,1,2,0:T(8,128)})) conditional(s32[]{:T(128)} %convert_element_type.260, (f32[2,1024,6]{1,2,0:T(8,128)S(1)}, f32[2,1024,6]{1,2,0:T(8,128)S(1)}, f32[2,1024,6,128]{3,1,2,0:T(8,128)}) %tuple.394, (pred[1024,1024]{0,1:T(8,128)(4,1)}, ...), branch_computations={%region_5.5_spmd, %region_6.8_spmd} | conditional | flops 6584033280 | bytes 177995872 | solution.py:38
  617.5 23.9 %multiply_add_fusion = f32[2,1024,6,128]{3,1,2,0:T(8,128)} fusion(f32[2,1024,6,128]{3,1,2,0:T(8,128)} %get-tuple-element.980, f32[2,1024,6]{1,2,0:T(8,128)S(1)} %get-tuple-element.1330, f32[2,1024,6,1024]{1,3,2,0:T(8,128)} %get-tuple-element.1394, f32[2,1024,6]{1,2,0:T(8,128)S(1)} %max.32, pred[1024,1024]{0,1:T(8,128)(4,1)S(1)} %copy-done.5, ...), kind=kOutput, calls=%fused_computation.8 | convolution fusion | flops 3274702848 | bytes 64585728 | tf_op jit(solution)/shard_map/while/body/eval_jaxpr/while/body/eval_jaxpr/cond/branch_1_fun/gqjk,kgd->gqjd/dot_general | solution.py:18
  646.4 69.2 %conditional.46 = ((f32[2,1024,6]{1,2,0:T(8,128)S(1)}, f32[2,1024,6]{1,2,0:T(8,128)S(1)}, f32[2,1024,6,128]{3,1,2,0:T(8,128)})) conditional(s32[]{:T(128)} %convert_element_type.262, (f32[2,1024,6]{1,2,0:T(8,128)S(1)}, f32[2,1024,6]{1,2,0:T(8,128)S(1)}, f32[2,1024,6,128]{3,1,2,0:T(8,128)}) %get-tuple-element.1908, (pred[1024,1024]{0,1:T(8,128)(4,1)}, ...), branch_computations={%region_33.33_spmd, %region_34.36_spmd} | conditional | flops 6584033280 | bytes 177995872 | solution.py:38
  691.7 23.9 %multiply_add_fusion.12 = f32[2,1024,6,128]{3,1,2,0:T(8,128)} fusion(f32[2,1024,6,128]{3,1,2,0:T(8,128)} %get-tuple-element.1022, f32[2,1024,6]{1,2,0:T(8,128)S(1)} %get-tuple-element.1342, f32[2,1024,6,1024]{1,3,2,0:T(8,128)} %get-tuple-element.1406, f32[2,1024,6]{1,2,0:T(8,128)S(1)} %max.38, pred[1024,1024]{0,1:T(8,128)(4,1)S(1)} %copy-done.3, ...), kind=kOutput, calls=%fused_computation.92 | convolution fusion | flops 3274702848 | bytes 64585728 | tf_op jit(solution)/shard_map/while/body/eval_jaxpr/cond/branch_1_fun/gqjk,kgd->gqjd/dot_general | solution.py:18
  715.9 73.5 %conditional.42 = ((f32[2,1024,6]{1,2,0:T(8,128)S(1)}, f32[2,1024,6]{1,2,0:T(8,128)S(1)}, f32[2,1024,6,128]{3,1,2,0:T(8,128)})) conditional(s32[]{:T(128)} %convert_element_type.258, (f32[2,1024,6]{1,2,0:T(8,128)S(1)}, f32[2,1024,6]{1,2,0:T(8,128)S(1)}, f32[2,1024,6,128]{3,1,2,0:T(8,128)}) %get-tuple-element.1904, (pred[1024,1024]{0,1:T(8,128)(4,1)}, ...), branch_computations={%region_13.13_spmd, %region_14.16_spmd} | conditional | flops 6584033280 | bytes 177995872 | solution.py:38
  765.5 23.9 %multiply_add_fusion.4 = f32[2,1024,6,128]{3,1,2,0:T(8,128)} fusion(f32[2,1024,6,128]{3,1,2,0:T(8,128)} %get-tuple-element.994, f32[2,1024,6]{1,2,0:T(8,128)S(1)} %get-tuple-element.1334, f32[2,1024,6,1024]{1,3,2,0:T(8,128)} %get-tuple-element.1398, f32[2,1024,6]{1,2,0:T(8,128)S(1)} %max.34, pred[1024,1024]{0,1:T(8,128)(4,1)S(1)} %copy-done.1, ...), kind=kOutput, calls=%fused_computation.36 | convolution fusion | flops 3274702848 | bytes 64585728 | tf_op jit(solution)/shard_map/while/body/eval_jaxpr/cond/branch_1_fun/gqjk,kgd->gqjd/dot_general | solution.py:18
  852.6 67.1 %conditional.44 = ((f32[2,1024,6]{1,2,0:T(8,128)S(1)}, f32[2,1024,6]{1,2,0:T(8,128)S(1)}, f32[2,1024,6,128]{3,1,2,0:T(8,128)})) conditional(s32[]{:T(128)} %convert_element_type.264, (f32[2,1024,6]{1,2,0:T(8,128)S(1)}, f32[2,1024,6]{1,2,0:T(8,128)S(1)}, f32[2,1024,6,128]{3,1,2,0:T(8,128)}) %tuple.310, (pred[1024,1024]{0,1:T(8,128)(4,1)}, ...), branch_computations={%region_25.25_spmd, %region_26.0_spmd} | conditional | flops 6584033280 | bytes 177995872 | solution.py:38
  920.6 72.9 %conditional.40 = ((f32[2,1024,6]{1,2,0:T(8,128)S(1)}, f32[2,1024,6]{1,2,0:T(8,128)S(1)}, f32[2,1024,6,128]{3,1,2,0:T(8,128)})) conditional(s32[]{:T(128)} %convert_element_type.260, (f32[2,1024,6]{1,2,0:T(8,128)S(1)}, f32[2,1024,6]{1,2,0:T(8,128)S(1)}, f32[2,1024,6,128]{3,1,2,0:T(8,128)}) %tuple.394, (pred[1024,1024]{0,1:T(8,128)(4,1)}, ...), branch_computations={%region_5.5_spmd, %region_6.8_spmd} | conditional | flops 6584033280 | bytes 177995872 | solution.py:38
  969.6 23.9 %multiply_add_fusion = f32[2,1024,6,128]{3,1,2,0:T(8,128)} fusion(f32[2,1024,6,128]{3,1,2,0:T(8,128)} %get-tuple-element.980, f32[2,1024,6]{1,2,0:T(8,128)S(1)} %get-tuple-element.1330, f32[2,1024,6,1024]{1,3,2,0:T(8,128)} %get-tuple-element.1394, f32[2,1024,6]{1,2,0:T(8,128)S(1)} %max.32, pred[1024,1024]{0,1:T(8,128)(4,1)S(1)} %copy-done.5, ...), kind=kOutput, calls=%fused_computation.8 | convolution fusion | flops 3274702848 | bytes 64585728 | tf_op jit(solution)/shard_map/while/body/eval_jaxpr/while/body/eval_jaxpr/cond/branch_1_fun/gqjk,kgd->gqjd/dot_general | solution.py:18
  998.3 69.5 %conditional.46 = ((f32[2,1024,6]{1,2,0:T(8,128)S(1)}, f32[2,1024,6]{1,2,0:T(8,128)S(1)}, f32[2,1024,6,128]{3,1,2,0:T(8,128)})) conditional(s32[]{:T(128)} %convert_element_type.262, (f32[2,1024,6]{1,2,0:T(8,128)S(1)}, f32[2,1024,6]{1,2,0:T(8,128)S(1)}, f32[2,1024,6,128]{3,1,2,0:T(8,128)}) %get-tuple-element.1908, (pred[1024,1024]{0,1:T(8,128)(4,1)}, ...), branch_computations={%region_33.33_spmd, %region_34.36_spmd} | conditional | flops 6584033280 | bytes 177995872 | solution.py:38
  1043.8 23.9 %multiply_add_fusion.12 = f32[2,1024,6,128]{3,1,2,0:T(8,128)} fusion(f32[2,1024,6,128]{3,1,2,0:T(8,128)} %get-tuple-element.1022, f32[2,1024,6]{1,2,0:T(8,128)S(1)} %get-tuple-element.1342, f32[2,1024,6,1024]{1,3,2,0:T(8,128)} %get-tuple-element.1406, f32[2,1024,6]{1,2,0:T(8,128)S(1)} %max.38, pred[1024,1024]{0,1:T(8,128)(4,1)S(1)} %copy-done.3, ...), kind=kOutput, calls=%fused_computation.92 | convolution fusion | flops 3274702848 | bytes 64585728 | tf_op jit(solution)/shard_map/while/body/eval_jaxpr/cond/branch_1_fun/gqjk,kgd->gqjd/dot_general | solution.py:18
  1068.0 73.3 %conditional.42 = ((f32[2,1024,6]{1,2,0:T(8,128)S(1)}, f32[2,1024,6]{1,2,0:T(8,128)S(1)}, f32[2,1024,6,128]{3,1,2,0:T(8,128)})) conditional(s32[]{:T(128)} %convert_element_type.258, (f32[2,1024,6]{1,2,0:T(8,128)S(1)}, f32[2,1024,6]{1,2,0:T(8,128)S(1)}, f32[2,1024,6,128]{3,1,2,0:T(8,128)}) %get-tuple-element.1904, (pred[1024,1024]{0,1:T(8,128)(4,1)}, ...), branch_computations={%region_13.13_spmd, %region_14.16_spmd} | conditional | flops 6584033280 | bytes 177995872 | solution.py:38
  1117.4 23.9 %multiply_add_fusion.4 = f32[2,1024,6,128]{3,1,2,0:T(8,128)} fusion(f32[2,1024,6,128]{3,1,2,0:T(8,128)} %get-tuple-element.994, f32[2,1024,6]{1,2,0:T(8,128)S(1)} %get-tuple-element.1334, f32[2,1024,6,1024]{1,3,2,0:T(8,128)} %get-tuple-element.1398, f32[2,1024,6]{1,2,0:T(8,128)S(1)} %max.34, pred[1024,1024]{0,1:T(8,128)(4,1)S(1)} %copy-done.1, ...), kind=kOutput, calls=%fused_computation.36 | convolution fusion | flops 3274702848 | bytes 64585728 | tf_op jit(solution)/shard_map/while/body/eval_jaxpr/cond/branch_1_fun/gqjk,kgd->gqjd/dot_general | solution.py:18
  1183.8 67.8 %conditional.16 = ((f32[2,1024,6]{1,2,0:T(8,128)}, f32[2,1024,6]{1,2,0:T(8,128)}, f32[2,1024,6,128]{3,1,2,0:T(8,128)})) conditional(s32[]{:T(128)} %convert_element_type.172, (f32[2,1024,6]{1,2,0:T(8,128)}, f32[2,1024,6]{1,2,0:T(8,128)}, f32[2,1024,6,128]{3,1,2,0:T(8,128)}) %tuple.139, (pred[1024,1024]{0,1:T(8,128)(4,1)}, ...), branch_computations={%region_46.47_spmd, %region_47.50_spmd} | conditional | flops 6584033280 | bytes 178585792 | solution.py:38
  1227.1 23.9 %multiply_add_fusion.16 = f32[2,1024,6,128]{3,1,2,0:T(8,128)} fusion(f32[2,1024,6,128]{3,1,2,0:T(8,128)} %get-tuple-element.1079, f32[2,1024,6]{1,2,0:T(8,128)S(1)} %get-tuple-element.1346, f32[2,1024,6,1024]{1,3,2,0:T(8,128)} %get-tuple-element.1410, f32[2,1024,6]{1,2,0:T(8,128)S(1)} %max.40, pred[1024,1024]{0,1:T(8,128)(4,1)S(1)} %copy-done.27, ...), kind=kOutput, calls=%fused_computation.120 | convolution fusion | flops 3274702848 | bytes 64585728 | tf_op jit(solution)/shard_map/while/body/eval_jaxpr/cond/branch_1_fun/gqjk,kgd->gqjd/dot_general | solution.py:18
  1258.6 66.6 %conditional.20 = ((f32[2,1024,6]{1,2,0:T(8,128)S(1)}, f32[2,1024,6]{1,2,0:T(8,128)S(1)}, f32[2,1024,6,128]{3,1,2,0:T(8,128)})) conditional(s32[]{:T(128)} %convert_element_type.176, (f32[2,1024,6]{1,2,0:T(8,128)S(1)}, f32[2,1024,6]{1,2,0:T(8,128)S(1)}, f32[2,1024,6,128]{3,1,2,0:T(8,128)}) %tuple.145, (pred[1024,1024]{0,1:T(8,128)(4,1)}, ...), branch_computations={%region_66.67_spmd, %region_67.70_spmd} | conditional | flops 6584033280 | bytes 177995872 | solution.py:38
  1301.3 23.9 %multiply_add_fusion.24 = f32[2,1024,6,128]{3,1,2,0:T(8,128)} fusion(f32[2,1024,6,128]{3,1,2,0:T(8,128)} %get-tuple-element.1107, f32[2,1024,6]{1,2,0:T(8,128)S(1)} %get-tuple-element.1354, f32[2,1024,6,1024]{1,3,2,0:T(8,128)} %get-tuple-element.1418, f32[2,1024,6]{1,2,0:T(8,128)S(1)} %max.44, pred[1024,1024]{0,1:T(8,128)(4,1)S(1)} %copy-done.25, ...), kind=kOutput, calls=%fused_computation.176 | convolution fusion | flops 3274702848 | bytes 64585728 | tf_op jit(solution)/shard_map/while/body/eval_jaxpr/cond/branch_1_fun/gqjk,kgd->gqjd/dot_general | solution.py:18
  1330.1 69.5 %conditional.18 = ((f32[2,1024,6]{1,2,0:T(8,128)S(1)}, f32[2,1024,6]{1,2,0:T(8,128)S(1)}, f32[2,1024,6,128]{3,1,2,0:T(8,128)})) conditional(s32[]{:T(128)} %convert_element_type.170, (f32[2,1024,6]{1,2,0:T(8,128)S(1)}, f32[2,1024,6]{1,2,0:T(8,128)S(1)}, f32[2,1024,6,128]{3,1,2,0:T(8,128)}) %tuple.400, (pred[1024,1024]{0,1:T(8,128)(4,1)}, ...), branch_computations={%region_54.55_spmd, %region_55.0_spmd} | conditional | flops 6584033280 | bytes 177995872 | solution.py:38
  1375.6 23.9 %multiply_add_fusion.20 = f32[2,1024,6,128]{3,1,2,0:T(8,128)} fusion(f32[2,1024,6,128]{3,1,2,0:T(8,128)} %get-tuple-element.1093, f32[2,1024,6]{1,2,0:T(8,128)S(1)} %get-tuple-element.1350, f32[2,1024,6,1024]{1,3,2,0:T(8,128)} %get-tuple-element.1414, f32[2,1024,6]{1,2,0:T(8,128)S(1)} %max.42, pred[1024,1024]{0,1:T(8,128)(4,1)S(1)} %copy-done.23, ...), kind=kOutput, calls=%fused_computation.148 | convolution fusion | flops 3274702848 | bytes 64585728 | tf_op jit(solution)/shard_map/cond/branch_1_fun/gqjk,kgd->gqjd/dot_general | solution.py:18
  1405.9 67.2 %conditional.22 = ((f32[2,1024,6]{1,2,0:T(8,128)S(1)}, f32[2,1024,6]{1,2,0:T(8,128)S(1)}, f32[2,1024,6,128]{3,1,2,0:T(8,128)})) conditional(s32[]{:T(128)} %convert_element_type.174, (f32[2,1024,6]{1,2,0:T(8,128)S(1)}, f32[2,1024,6]{1,2,0:T(8,128)S(1)}, f32[2,1024,6,128]{3,1,2,0:T(8,128)}) %get-tuple-element.1900, (pred[1024,1024]{0,1:T(8,128)(4,1)}, ...), branch_computations={%region_74.75_spmd, %region_75.0_spmd} | conditional | flops 6584033280 | bytes 177995872 | solution.py:38
  (311 shorter events, 1045.6 us)
Async XLA Ops:
  23.6 266.2 %collective-permute-start.4 = (bf16[2048,2,128]{2,0,1:T(8,128)(2,1)}, bf16[2048,2,128]{2,0,1:T(8,128)(2,1)}, u32[]{:S(2)}, u32[]{:S(2)}) collective-permute-start(bf16[2048,2,128]{2,0,1:T(8,128)(2,1)} %copy.151), channel_id=1, source_target_pairs={{0,4},{4,0},{1,5},{5,1},{2,6},{6,2},{3,7},{7,3}} | collective-permute-start | bytes 3145736 | tf_op jit(solution)/shard_map/while/body/eval_jaxpr/while/body/eval_jaxpr/ppermute | solution.py:75
  23.8 413.8 %collective-permute-start = (bf16[2048,2,128]{2,0,1:T(8,128)(2,1)}, bf16[2048,2,128]{2,0,1:T(8,128)(2,1)}, u32[]{:S(2)}, u32[]{:S(2)}) collective-permute-start(bf16[2048,2,128]{2,0,1:T(8,128)(2,1)} %copy.151), channel_id=1, source_target_pairs={{0,1},{1,2},{2,3},{3,0},{4,5},{5,6},{6,7},{7,4}} | collective-permute-start | bytes 3145736 | tf_op jit(solution)/shard_map/while/body/eval_jaxpr/ppermute | solution.py:83
  26.7 265.4 %collective-permute-start.5 = (bf16[2048,2,128]{2,0,1:T(8,128)(2,1)}, bf16[2048,2,128]{2,0,1:T(8,128)(2,1)}, u32[]{:S(2)}, u32[]{:S(2)}) collective-permute-start(bf16[2048,2,128]{2,0,1:T(8,128)(2,1)} %copy.152), channel_id=1, source_target_pairs={{0,4},{4,0},{1,5},{5,1},{2,6},{6,2},{3,7},{7,3}} | collective-permute-start | bytes 3145736 | tf_op jit(solution)/shard_map/while/body/eval_jaxpr/while/body/eval_jaxpr/ppermute | solution.py:75
  28.4 409.2 %collective-permute-start.1 = (bf16[2048,2,128]{2,0,1:T(8,128)(2,1)}, bf16[2048,2,128]{2,0,1:T(8,128)(2,1)}, u32[]{:S(2)}, u32[]{:S(2)}) collective-permute-start(bf16[2048,2,128]{2,0,1:T(8,128)(2,1)} %copy.152), channel_id=1, source_target_pairs={{0,1},{1,2},{2,3},{3,0},{4,5},{5,6},{6,7},{7,4}} | collective-permute-start | bytes 3145736 | tf_op jit(solution)/shard_map/while/body/eval_jaxpr/ppermute | solution.py:83
  30.0 40.6 %collective-permute-start.3 = (s32[2048]{0:T(1024)}, s32[2048]{0:T(1024)S(1)}, u32[]{:S(2)}, u32[]{:S(2)}) collective-permute-start(s32[2048]{0:T(1024)} %copy.153), channel_id=1, source_target_pairs={{0,4},{4,0},{1,5},{5,1},{2,6},{6,2},{3,7},{7,3}} | collective-permute-start | bytes 24584 | tf_op jit(solution)/shard_map/while/body/eval_jaxpr/while/body/eval_jaxpr/ppermute | solution.py:75
  70.6 367.1 %collective-permute-start.2 = (s32[2048]{0:T(1024)}, s32[2048]{0:T(1024)}, u32[]{:S(2)}, u32[]{:S(2)}) collective-permute-start(s32[2048]{0:T(1024)} %copy.153), channel_id=1, source_target_pairs={{0,1},{1,2},{2,3},{3,0},{4,5},{5,6},{6,7},{7,4}} | collective-permute-start | bytes 24584 | tf_op jit(solution)/shard_map/while/body/eval_jaxpr/ppermute | solution.py:83
  109.7 21.5 %copy-start.34 = (bf16[1024,2,128]{2,0,1:T(8,128)(2,1)S(1)}, bf16[1024,2,128]{2,0,1:T(8,128)(2,1)}, u32[]{:S(2)}) copy-start(bf16[1024,2,128]{2,0,1:T(8,128)(2,1)} %get-tuple-element.1009) | copy-start | bytes 1572868 | tf_op jit(solution)/shard_map/while/body/eval_jaxpr/while/body/eval_jaxpr/cond
  155.2 67.3 %copy-start.8 = (f32[2,1024,6]{1,2,0:T(8,128)S(1)}, f32[2,1024,6]{1,2,0:T(8,128)}, u32[]{:S(2)}) copy-start(f32[2,1024,6]{1,2,0:T(8,128)} %get-tuple-element.1805) | copy-start | bytes 147460 | tf_op jit(solution)/shard_map/while
  155.2 67.3 %copy-start.13 = (f32[2,1024,6]{1,2,0:T(8,128)S(1)}, f32[2,1024,6]{1,2,0:T(8,128)}, u32[]{:S(2)}) copy-start(f32[2,1024,6]{1,2,0:T(8,128)} %get-tuple-element.1806) | copy-start | bytes 147460 | tf_op jit(solution)/shard_map/while
  448.3 193.6 %collective-permute-start.4 = (bf16[2048,2,128]{2,0,1:T(8,128)(2,1)}, bf16[2048,2,128]{2,0,1:T(8,128)(2,1)}, u32[]{:S(2)}, u32[]{:S(2)}) collective-permute-start(bf16[2048,2,128]{2,0,1:T(8,128)(2,1)} %copy.151), channel_id=1, source_target_pairs={{0,4},{4,0},{1,5},{5,1},{2,6},{6,2},{3,7},{7,3}} | collective-permute-start | bytes 3145736 | tf_op jit(solution)/shard_map/while/body/eval_jaxpr/while/body/eval_jaxpr/ppermute | solution.py:75
  448.3 341.4 %collective-permute-start = (bf16[2048,2,128]{2,0,1:T(8,128)(2,1)}, bf16[2048,2,128]{2,0,1:T(8,128)(2,1)}, u32[]{:S(2)}, u32[]{:S(2)}) collective-permute-start(bf16[2048,2,128]{2,0,1:T(8,128)(2,1)} %copy.151), channel_id=1, source_target_pairs={{0,1},{1,2},{2,3},{3,0},{4,5},{5,6},{6,7},{7,4}} | collective-permute-start | bytes 3145736 | tf_op jit(solution)/shard_map/while/body/eval_jaxpr/ppermute | solution.py:83
  450.6 193.6 %collective-permute-start.5 = (bf16[2048,2,128]{2,0,1:T(8,128)(2,1)}, bf16[2048,2,128]{2,0,1:T(8,128)(2,1)}, u32[]{:S(2)}, u32[]{:S(2)}) collective-permute-start(bf16[2048,2,128]{2,0,1:T(8,128)(2,1)} %copy.152), channel_id=1, source_target_pairs={{0,4},{4,0},{1,5},{5,1},{2,6},{6,2},{3,7},{7,3}} | collective-permute-start | bytes 3145736 | tf_op jit(solution)/shard_map/while/body/eval_jaxpr/while/body/eval_jaxpr/ppermute | solution.py:75
  452.1 337.6 %collective-permute-start.1 = (bf16[2048,2,128]{2,0,1:T(8,128)(2,1)}, bf16[2048,2,128]{2,0,1:T(8,128)(2,1)}, u32[]{:S(2)}, u32[]{:S(2)}) collective-permute-start(bf16[2048,2,128]{2,0,1:T(8,128)(2,1)} %copy.152), channel_id=1, source_target_pairs={{0,1},{1,2},{2,3},{3,0},{4,5},{5,6},{6,7},{7,4}} | collective-permute-start | bytes 3145736 | tf_op jit(solution)/shard_map/while/body/eval_jaxpr/ppermute | solution.py:83
  453.4 31.5 %collective-permute-start.3 = (s32[2048]{0:T(1024)}, s32[2048]{0:T(1024)S(1)}, u32[]{:S(2)}, u32[]{:S(2)}) collective-permute-start(s32[2048]{0:T(1024)} %copy.153), channel_id=1, source_target_pairs={{0,4},{4,0},{1,5},{5,1},{2,6},{6,2},{3,7},{7,3}} | collective-permute-start | bytes 24584 | tf_op jit(solution)/shard_map/while/body/eval_jaxpr/while/body/eval_jaxpr/ppermute | solution.py:75
  484.9 304.8 %collective-permute-start.2 = (s32[2048]{0:T(1024)}, s32[2048]{0:T(1024)}, u32[]{:S(2)}, u32[]{:S(2)}) collective-permute-start(s32[2048]{0:T(1024)} %copy.153), channel_id=1, source_target_pairs={{0,1},{1,2},{2,3},{3,0},{4,5},{5,6},{6,7},{7,4}} | collective-permute-start | bytes 24584 | tf_op jit(solution)/shard_map/while/body/eval_jaxpr/ppermute | solution.py:83
  522.4 21.5 %copy-start.34 = (bf16[1024,2,128]{2,0,1:T(8,128)(2,1)S(1)}, bf16[1024,2,128]{2,0,1:T(8,128)(2,1)}, u32[]{:S(2)}) copy-start(bf16[1024,2,128]{2,0,1:T(8,128)(2,1)} %get-tuple-element.1009) | copy-start | bytes 1572868 | tf_op jit(solution)/shard_map/while/body/eval_jaxpr/while/body/eval_jaxpr/cond
  800.2 193.6 %collective-permute-start.4 = (bf16[2048,2,128]{2,0,1:T(8,128)(2,1)}, bf16[2048,2,128]{2,0,1:T(8,128)(2,1)}, u32[]{:S(2)}, u32[]{:S(2)}) collective-permute-start(bf16[2048,2,128]{2,0,1:T(8,128)(2,1)} %copy.151), channel_id=1, source_target_pairs={{0,4},{4,0},{1,5},{5,1},{2,6},{6,2},{3,7},{7,3}} | collective-permute-start | bytes 3145736 | tf_op jit(solution)/shard_map/while/body/eval_jaxpr/while/body/eval_jaxpr/ppermute | solution.py:75
  800.2 341.6 %collective-permute-start = (bf16[2048,2,128]{2,0,1:T(8,128)(2,1)}, bf16[2048,2,128]{2,0,1:T(8,128)(2,1)}, u32[]{:S(2)}, u32[]{:S(2)}) collective-permute-start(bf16[2048,2,128]{2,0,1:T(8,128)(2,1)} %copy.151), channel_id=1, source_target_pairs={{0,1},{1,2},{2,3},{3,0},{4,5},{5,6},{6,7},{7,4}} | collective-permute-start | bytes 3145736 | tf_op jit(solution)/shard_map/while/body/eval_jaxpr/ppermute | solution.py:83
  802.5 193.6 %collective-permute-start.5 = (bf16[2048,2,128]{2,0,1:T(8,128)(2,1)}, bf16[2048,2,128]{2,0,1:T(8,128)(2,1)}, u32[]{:S(2)}, u32[]{:S(2)}) collective-permute-start(bf16[2048,2,128]{2,0,1:T(8,128)(2,1)} %copy.152), channel_id=1, source_target_pairs={{0,4},{4,0},{1,5},{5,1},{2,6},{6,2},{3,7},{7,3}} | collective-permute-start | bytes 3145736 | tf_op jit(solution)/shard_map/while/body/eval_jaxpr/while/body/eval_jaxpr/ppermute | solution.py:75
  803.9 337.9 %collective-permute-start.1 = (bf16[2048,2,128]{2,0,1:T(8,128)(2,1)}, bf16[2048,2,128]{2,0,1:T(8,128)(2,1)}, u32[]{:S(2)}, u32[]{:S(2)}) collective-permute-start(bf16[2048,2,128]{2,0,1:T(8,128)(2,1)} %copy.152), channel_id=1, source_target_pairs={{0,1},{1,2},{2,3},{3,0},{4,5},{5,6},{6,7},{7,4}} | collective-permute-start | bytes 3145736 | tf_op jit(solution)/shard_map/while/body/eval_jaxpr/ppermute | solution.py:83
  805.2 31.5 %collective-permute-start.3 = (s32[2048]{0:T(1024)}, s32[2048]{0:T(1024)S(1)}, u32[]{:S(2)}, u32[]{:S(2)}) collective-permute-start(s32[2048]{0:T(1024)} %copy.153), channel_id=1, source_target_pairs={{0,4},{4,0},{1,5},{5,1},{2,6},{6,2},{3,7},{7,3}} | collective-permute-start | bytes 24584 | tf_op jit(solution)/shard_map/while/body/eval_jaxpr/while/body/eval_jaxpr/ppermute | solution.py:75
  836.7 305.1 %collective-permute-start.2 = (s32[2048]{0:T(1024)}, s32[2048]{0:T(1024)}, u32[]{:S(2)}, u32[]{:S(2)}) collective-permute-start(s32[2048]{0:T(1024)} %copy.153), channel_id=1, source_target_pairs={{0,1},{1,2},{2,3},{3,0},{4,5},{5,6},{6,7},{7,4}} | collective-permute-start | bytes 24584 | tf_op jit(solution)/shard_map/while/body/eval_jaxpr/ppermute | solution.py:83
  874.3 21.5 %copy-start.34 = (bf16[1024,2,128]{2,0,1:T(8,128)(2,1)S(1)}, bf16[1024,2,128]{2,0,1:T(8,128)(2,1)}, u32[]{:S(2)}) copy-start(bf16[1024,2,128]{2,0,1:T(8,128)(2,1)} %get-tuple-element.1009) | copy-start | bytes 1572868 | tf_op jit(solution)/shard_map/while/body/eval_jaxpr/while/body/eval_jaxpr/cond
  1157.9 10.1 collective-permute-start.6
  1157.9 167.6 %collective-permute-start.8 = (bf16[2048,2,128]{2,0,1:T(8,128)(2,1)}, bf16[2048,2,128]{2,0,1:T(8,128)(2,1)}, u32[]{:S(2)}, u32[]{:S(2)}) collective-permute-start(bf16[2048,2,128]{2,0,1:T(8,128)(2,1)} %get-tuple-element.1166), channel_id=1, source_target_pairs={{0,4},{4,0},{1,5},{5,1},{2,6},{6,2},{3,7},{7,3}} | collective-permute-start | bytes 3145736 | tf_op jit(solution)/shard_map/while/body/eval_jaxpr/ppermute | solution.py:75
  1159.4 168.4 %collective-permute-start.7 = (bf16[2048,2,128]{2,0,1:T(8,128)(2,1)}, bf16[2048,2,128]{2,0,1:T(8,128)(2,1)}, u32[]{:S(2)}, u32[]{:S(2)}) collective-permute-start(bf16[2048,2,128]{2,0,1:T(8,128)(2,1)} %get-tuple-element.1165), channel_id=1, source_target_pairs={{0,4},{4,0},{1,5},{5,1},{2,6},{6,2},{3,7},{7,3}} | collective-permute-start | bytes 3145736 | tf_op jit(solution)/shard_map/while/body/eval_jaxpr/ppermute | solution.py:75
  1183.9 21.7 %copy-start.10 = (f32[2,1024,6]{1,2,0:T(8,128)S(1)}, f32[2,1024,6]{1,2,0:T(8,128)}, u32[]{:S(2)}) copy-start(f32[2,1024,6]{1,2,0:T(8,128)} %get-tuple-element.1074) | copy-start | bytes 147460 | tf_op jit(solution)/shard_map/while/body/eval_jaxpr/cond
  1183.9 43.1 %copy-start.15 = (f32[2,1024,6]{1,2,0:T(8,128)S(1)}, f32[2,1024,6]{1,2,0:T(8,128)}, u32[]{:S(2)}) copy-start(f32[2,1024,6]{1,2,0:T(8,128)} %get-tuple-element.1078) | copy-start | bytes 147460 | tf_op jit(solution)/shard_map/while/body/eval_jaxpr/cond
  1205.5 21.5 %copy-start.27 = (pred[1024,1024]{0,1:T(8,128)(4,1)S(1)}, pred[1024,1024]{0,1:T(8,128)(4,1)}, u32[]{:S(2)}) copy-start(pred[1024,1024]{0,1:T(8,128)(4,1)} %get-tuple-element.1075) | copy-start | bytes 3145732 | tf_op jit(solution)/shard_map/while/body/eval_jaxpr/cond
  1205.5 21.6 %copy-start.42 = (bf16[1024,2,128]{2,0,1:T(8,128)(2,1)S(1)}, bf16[1024,2,128]{2,0,1:T(8,128)(2,1)}, u32[]{:S(2)}) copy-start(bf16[1024,2,128]{2,0,1:T(8,128)(2,1)} %get-tuple-element.1080) | copy-start | bytes 1572868 | tf_op jit(solution)/shard_map/while/body/eval_jaxpr/cond
  1227.1 24.6 %copy-start.16 = (f32[2,1024,6]{1,2,0:T(8,128)}, f32[2,1024,6]{1,2,0:T(8,128)S(1)}, u32[]{:S(2)}) copy-start(f32[2,1024,6]{1,2,0:T(8,128)S(1)} %get-tuple-element.1877) | copy-start | bytes 147460 | tf_op jit(solution)/shard_map/while/body/eval_jaxpr/cond
  1427.6 21.5 %copy-start.39 = (bf16[1024,2,128]{2,0,1:T(8,128)(2,1)S(1)}, bf16[1024,2,128]{2,0,1:T(8,128)(2,1)}, u32[]{:S(2)}) copy-start(bf16[1024,2,128]{2,0,1:T(8,128)(2,1)} %get-tuple-element.1122) | copy-start | bytes 1572868 | tf_op jit(solution)/shard_map/cond
  (40 other events, 619.4 us)
where the time goes:
time: 1490 us; the launch traced here: 1480 us
  matrix products  770 us (52%)
  other arithmetic  423 us (28%)
  loops' own time  101 us (7%)
  local copies, waits for them, and re-layouts  98.1 us (7%)
  waiting for transfers between devices  77.7 us (5%)
    dot_general x17, matrix products, piece_update(): jnp.einsum('gqjk,kgd->gqjd', weights.astype(jnp.bfloat16), v_piece, prefe...  407 us
    reduce_sum x17, other arithmetic, piece_update(): sum_new = sum_old * rescale + jnp.sum(weights, axis=-1)  365 us
    dot_general x17, matrix products, piece_update(): jnp.einsum('qgjd,kgd->gqjk', q_piece, k_piece, preferred_element_type=jnp...  364 us
    ppermute x12, waiting for transfers between devices, inner_body(): lax.ppermute(block_arr, 'cy', cy_perm)  77.7 us
    another operation x32, loops' own time, block_update(): lax.cond(jnp.any(allowed), piece_update, keep_stats, cur_stats, q_pieces[...  54.5 us
    another operation x1, loops' own time, per_device(): lax.fori_loop(0, size_cx - 1, outer_body, ((k_loc, v_loc, doc_loc), (fres...  46.3 us
    reduce_or x4, other arithmetic, block_update(): jnp.any(allowed)  44 us
  transfers between devices with their start and end apart: 21, of which 3 were waited for; matrix products, arithmetic and copies ran while one was open for 75% of the time, Pallas kernels for 0%

commit v1 on v0

v1 whole, which is shorter than its diff:
```python
import functools

import jax
import jax.numpy as jnp
from jax import lax
from jax.experimental import pallas as pl
from jax.experimental.pallas import tpu as pltpu
from jax.sharding import PartitionSpec as P

NEG_BIG = -1e30
LOG2E = 1.4426950408889634
DOCS = 6
TILE = 256
BLOCK = 512
CHUNK = 256
MAX_ITEMS = 256


def fold8(x, op):
    return op(x.reshape(x.shape[0] // 8, 8, x.shape[1]), axis=0)


def attend_kernel(
    masks, group, first_stage, last_stage,
    rank_ref, cnt_ref, qd_ref, qdoc_ref, q_hbm, k_hbm, v_hbm, *rest,
):
    n_in = 0 if first_stage else 3
    n_out = 1 if last_stage else 3
    state_in, rest = rest[:n_in], rest[n_in:]
    outs, rest = rest[:n_out], rest[n_out:]
    q_ref, k_ref, v_ref, s_ref, mx_ref, m_ref, l_ref, acc_ref, o_ref, it_tile, it_sp, it_start, it_mask, sems = rest
    n_src = len(masks)
    n_tiles, n_pairs = q_ref.shape[0], q_ref.shape[1]
    per_kv = n_pairs // 2
    piece = k_ref.shape[2] // 2
    tiles_per_piece = piece // TILE
    scale = q_ref.shape[-1] ** -0.5 * LOG2E
    rank = rank_ref[0]

    copies = [pltpu.make_async_copy(q_hbm, q_ref, sems.at[0])]
    copies += [pltpu.make_async_copy(k_hbm, k_ref, sems.at[1]), pltpu.make_async_copy(v_hbm, v_ref, sems.at[2])]
    if not first_stage:
        copies += [pltpu.make_async_copy(a, b, sems.at[3 + i]) for i, (a, b) in enumerate(zip(state_in, (m_ref, l_ref, acc_ref)))]
    for copy in copies:
        copy.start()

    def list_tile(tile, count):
        half = tile // tiles_per_piece
        off = (tile % tiles_per_piece) * TILE
        q_piece = jnp.where(half == 0, rank, 2 * group - 1 - rank)
        d_first, d_last = qd_ref[2 * tile], qd_ref[2 * tile + 1]
        for src in range(n_src):
            src_rank = rank ^ masks[src]
            for k_half in range(2):
                sp = 2 * src + k_half
                k_piece = src_rank if k_half == 0 else 2 * group - 1 - src_rank
                lo = cnt_ref[sp * DOCS + d_first]
                lo_last = cnt_ref[sp * DOCS + d_last]
                diag = k_piece == q_piece
                hi = jnp.where(diag, off + TILE, piece)
                need = jnp.where(jnp.logical_and(k_piece <= q_piece, lo < hi), hi - (lo // 128) * 128, 0)
                blocks = (need + BLOCK - 1) // BLOCK
                start0 = jnp.maximum(hi - BLOCK * blocks, 0)

                def add(i, at, sp=sp, start0=start0, diag=diag, lo_last=lo_last):
                    start = start0 + i * BLOCK
                    it_tile[at] = tile
                    it_sp[at] = sp
                    it_start[at] = start
                    cut = jnp.logical_or(start < lo_last, jnp.logical_and(diag, start + BLOCK > off + 1))
                    it_mask[at] = jnp.where(cut, jnp.where(diag, 2, 1), 0)
                    return at + 1

                count = lax.fori_loop(0, blocks, add, count)
        return count

    count = lax.fori_loop(0, n_tiles, list_tile, 0)

    if first_stage:
        m_ref[...] = jnp.full_like(m_ref, NEG_BIG)
        l_ref[...] = jnp.zeros_like(l_ref)
        acc_ref[...] = jnp.zeros_like(acc_ref)
    for copy in copies:
        copy.wait()

    def score_chunk(tile, sp, start, h, j):
        src, base = sp // 2, (sp % 2) * piece
        rows = pl.ds(pl.multiple_of(base + start + j * CHUNK, 128), CHUNK)
        return lax.dot_general(
            k_ref[src, h // per_kv, rows, :], q_ref[tile, h], (((1,), (1,)), ((), ())), preferred_element_type=jnp.float32
        )

    def values_chunk(sp, start, h, j):
        src, base = sp // 2, (sp % 2) * piece
        return v_ref[src, h // per_kv, :, pl.ds(pl.multiple_of(base + start + j * CHUNK, 128), CHUNK)]

    n_chunks = BLOCK // CHUNK

    @pl.when(count > 0)
    def prologue():
        for h in range(n_pairs):
            top = None
            for j in range(n_chunks):
                s = score_chunk(it_tile[0], it_sp[0], it_start[0], h, j)
                s_ref[h, j * CHUNK:(j + 1) * CHUNK, :] = s
                part = fold8(s, jnp.max)
                top = part if top is None else jnp.maximum(top, part)
            mx_ref[h] = top

    def body(t, masked):
        tile, sp, start = it_tile[t], it_sp[t], it_start[t]
        nxt = jnp.minimum(t + 1, count - 1)
        n_tile, n_sp, n_start = it_tile[nxt], it_sp[nxt], it_start[nxt]
        if masked:
            q_doc = qdoc_ref[tile]
            low = jnp.zeros_like(q_doc)
            for d in range(DOCS):
                low = jnp.where(q_doc == d, cnt_ref[sp * DOCS + d], low)
            off = (tile % tiles_per_piece) * TILE
            token = lax.broadcasted_iota(jnp.int32, q_doc.shape, 1) % TILE + off
            high = jnp.where(it_mask[t] == 2, token, piece)

            def allowed(j):
                k_idx = lax.broadcasted_iota(jnp.int32, (CHUNK, q_doc.shape[1]), 0) + (start + j * CHUNK)
                return jnp.logical_and(k_idx >= low, k_idx <= high)

        for h in range(n_pairs):
            if masked:
                top = None
                for j in range(n_chunks):
                    part = fold8(jnp.where(allowed(j), s_ref[h, j * CHUNK:(j + 1) * CHUNK, :], NEG_BIG), jnp.max)
                    top = part if top is None else jnp.maximum(top, part)
            else:
                top = mx_ref[h]
            m_old = m_ref[tile, h]
            m_new = jnp.maximum(m_old, jnp.max(top, axis=0, keepdims=True) * scale)
            rescale = jnp.exp2(m_old - m_new)
            m_ref[tile, h] = m_new
            total = l_ref[tile, h] * rescale
            part_acc = None
            new_top = None
            for j in range(n_chunks):
                p = jnp.exp2(s_ref[h, j * CHUNK:(j + 1) * CHUNK, :] * scale - m_new)
                if masked:
                    p = jnp.where(allowed(j), p, 0.0)
                total = total + fold8(p, jnp.sum)
                prod = jnp.dot(values_chunk(sp, start, h, j), p.astype(jnp.bfloat16), preferred_element_type=jnp.float32)
                part_acc = prod if part_acc is None else part_acc + prod
                s = score_chunk(n_tile, n_sp, n_start, h, j)
                s_ref[h, j * CHUNK:(j + 1) * CHUNK, :] = s
                part = fold8(s, jnp.max)
                new_top = part if new_top is None else jnp.maximum(new_top, part)
            mx_ref[h] = new_top
            l_ref[tile, h] = total
            acc_ref[tile, h] = acc_ref[tile, h] * rescale + part_acc

    def step(t, carry):
        masked = it_mask[t] > 0
        pl.when(masked)(lambda: body(t, True))
        pl.when(jnp.logical_not(masked))(lambda: body(t, False))
        return carry

    lax.fori_loop(0, count, step, 0)

    if last_stage:
        def finish(tile, carry):
            for h in range(n_pairs):
                denom = jnp.sum(l_ref[tile, h], axis=0, keepdims=True)
                o_ref[tile, h] = (acc_ref[tile, h] / denom).T.astype(o_ref.dtype)
            return carry

        lax.fori_loop(0, n_tiles, finish, 0)
        ends = [pltpu.make_async_copy(o_ref, outs[0], sems.at[0])]
    else:
        ends = [pltpu.make_async_copy(a, b, sems.at[i]) for i, (a, b) in enumerate(zip((m_ref, l_ref, acc_ref), outs))]
    for copy in ends:
        copy.start()
    for copy in ends:
        copy.wait()


def attend(masks, group, rank, cnt, qd, qdoc, q, k, v, state, last):
    n_tiles, n_pairs, cols, dim = q.shape
    stat = [(n_tiles, n_pairs, 1, cols), (n_tiles, n_pairs, 8, cols), (n_tiles, n_pairs, dim, cols)]
    if last:
        out_shape = [jax.ShapeDtypeStruct(q.shape, jnp.bfloat16)]
    else:
        out_shape = [jax.ShapeDtypeStruct(shape, jnp.float32) for shape in stat]
    state = () if state is None else tuple(state)
    any_spec = pl.BlockSpec(memory_space=pl.ANY)
    smem = pl.BlockSpec(memory_space=pltpu.SMEM)
    vmem = pl.BlockSpec(memory_space=pltpu.VMEM)
    items = 2 * n_tiles * 2 * len(masks)
    flops = len(masks) * 2 * 10**9
    return pl.pallas_call(
        functools.partial(attend_kernel, masks, group, not state, last),
        out_shape=out_shape,
        in_specs=[smem, smem, smem, vmem, any_spec, any_spec, any_spec] + [any_spec] * len(state),
        out_specs=[any_spec] * len(out_shape),
        scratch_shapes=[
            pltpu.VMEM(q.shape, q.dtype),
            pltpu.VMEM(k.shape, k.dtype),
            pltpu.VMEM(v.shape, v.dtype),
            pltpu.VMEM((n_pairs, BLOCK, cols), jnp.float32),
            pltpu.VMEM((n_pairs, 8, cols), jnp.float32),
            *[pltpu.VMEM(shape, jnp.float32) for shape in stat],
            pltpu.VMEM(q.shape if last else (8, 128), jnp.bfloat16),
            *[pltpu.SMEM((items,), jnp.int32)] * 4,
            pltpu.SemaphoreType.DMA((6,)),
        ],
        compiler_params=pltpu.CompilerParams(vmem_limit_bytes=60 * 1024 * 1024),
        cost_estimate=pl.CostEstimate(flops=flops, bytes_accessed=20 << 20, transcendentals=0),
    )(rank, cnt, qd, qdoc, q, k, v, *state)


def solution(mesh):
    size_cx, size_cy = mesh.shape['cx'], mesh.shape['cy']
    group = size_cx * size_cy
    seq_spec = P(('dp', 'cx', 'cy'), None, None)

    def per_device(q_loc, k_loc, v_loc, doc_loc):
        tok, heads, dim = q_loc.shape
        kv_heads = k_loc.shape[1]
        piece = tok // 2
        n_tiles = tok // TILE
        rank = lax.axis_index('cx') * size_cy + lax.axis_index('cy')
        q = q_loc.reshape(n_tiles, TILE, heads // 2, 2, dim).transpose(0, 2, 3, 1, 4).reshape(n_tiles, heads // 2, 2 * TILE, dim)
        k = k_loc.transpose(1, 0, 2)
        v = v_loc.transpose(1, 2, 0)
        doc_tiles = doc_loc.reshape(n_tiles, 1, TILE)
        qdoc = jnp.concatenate([doc_tiles, doc_tiles], axis=2)
        qd = jnp.stack([doc_tiles[:, 0, 0], doc_tiles[:, 0, -1]], axis=1).reshape(-1)
        cnt = jnp.sum(doc_loc.reshape(2, 1, piece) < jnp.arange(DOCS)[None, :, None], axis=-1).astype(jnp.int32)
        gather = functools.partial(lax.all_gather, axis_name=('cx', 'cy'))
        k_all, v_all, cnt_all = gather(k), gather(v), gather(cnt)
        order = jnp.arange(group) ^ rank
        cnt_all = cnt_all[order]
        k_all, v_all = k_all[order], v_all[order]
        out, = attend(tuple(range(group)), group, rank[None], cnt_all.reshape(-1), qd, qdoc, q, k_all, v_all, None, True)
        out = out.reshape(n_tiles, heads // 2, 2, TILE, dim).transpose(0, 3, 1, 2, 4)
        return out.reshape(tok, heads, dim)

    return jax.shard_map(per_device, mesh=mesh, in_specs=(seq_spec, seq_spec, seq_spec, P(('dp', 'cx', 'cy'))), out_specs=seq_spec, check_vma=False)
```

time: 1490 us -> 325 us (0.22)
  matrix products: 770 us -> 0 us
  other arithmetic: 423 us -> 0.82 us
  Pallas kernels: 0 us -> 194 us
  loops' own time: 101 us -> 0 us
  local copies, waits for them, and re-layouts: 98.1 us -> 38.9 us
    dot_general x34 -> x0, matrix products: 770 us -> none  [the longest x17 407 us: piece_update(): jnp.einsum('gqjk,kgd->gqjd', weights.astype(jnp.bfloat16), v_piece, prefe...]
    reduce_sum x17 -> x1, other arithmetic: 365 us -> 0.19 us  [per_device(): jnp.sum(doc_loc.reshape(2, 1, piece) < jnp.arange(DOCS)[None, :, None], a...]
    pallas_call x0 -> x1, Pallas kernels: none -> 194 us  [attend(): pl.pallas_call(functools.partial(attend_kernel, masks, group, not state,...]
    another operation x33 -> x0, loops' own time: 101 us -> none  [the longest x32 54.5 us: block_update(): lax.cond(jnp.any(allowed), piece_update, keep_stats, cur_stats, q_pieces[...]
    ppermute x21 -> x0, waiting for transfers between devices: 77.7 us -> none  [the longest x12 77.7 us: inner_body(): lax.ppermute(block_arr, 'cy', cy_perm)]
    all_gather x0 -> x2, waiting for transfers between devices: none -> 67.4 us  [per_device(): k_all, v_all, cnt_all = (gather(k), gather(v), gather(cnt))]
    reduce_or x4 -> x0, other arithmetic: 44 us -> none  [block_update(): jnp.any(allowed)]
    slice x22 -> x1, local copies, waits for them, and re-layouts: 38.8 us -> 1.11 us  [per_device(): doc_tiles[:, 0, 0]]
  transfers between devices with their start and end apart: 21 -> 2, of which waited for: 3 -> 2; matrix products, arithmetic and copies ran while one was open for 75% -> 7% of each run, Pallas kernels for 0% -> 0%
where the time goes in v1:
time: 325 us; the launch traced here: 324 us
  Pallas kernels  194 us (60%)
  waiting for transfers between devices  67.5 us (21%)
  local copies, waits for them, and re-layouts  38.9 us (12%)
  between operations  13.4 us (4%)
  blocking collectives  9.38 us (3%)
    pallas_call x1, Pallas kernels, attend(): pl.pallas_call(functools.partial(attend_kernel, masks, group, not state,...  194 us
    all_gather x2, waiting for transfers between devices, per_device(): k_all, v_all, cnt_all = (gather(k), gather(v), gather(cnt))  67.4 us
    gather x2, local copies, waits for them, and re-layouts, per_device(): k_all, v_all = (k_all[order], v_all[order])  16.3 us
    all_gather x1, blocking collectives, per_device(): k_all, v_all, cnt_all = (gather(k), gather(v), gather(cnt))  9.38 us
  transfers between devices with their start and end apart: 2, of which 2 were waited for; matrix products, arithmetic and copies ran while one was open for 7% of the time, Pallas kernels for 0%

profile of v1, /device:TPU:7, one launch (start us, length us, event | category | flops | bytes accessed | tf_op | source)
XLA Modules:
  0.0 324.2 jit_solution(5273334847975971778)
XLA Ops:
  6.5 0.0 all-gather.7.cloned.1.call-start
  6.5 2.4 copy.25
  9.0 0.0 copy-start
  9.0 0.0 all-gather.7.cloned.1.call-update
  9.0 0.0 all-gather.9.cloned.1.call-start
  9.0 3.7 %copy.22 = bf16[2048,2,128]{0,2,1:T(8,128)(2,1)} copy(bf16[2048,2,128]{2,1,0:T(2,128)(2,1)} %param.6) | data formatting | bytes 2097152 | tf_op args[2]
  12.8 0.0 all-gather.9.cloned.1.call-update
  12.8 0.7 lt.27
  13.5 1.1 slice_reduce_fusion.1
  14.6 0.1 copy.19
  14.7 0.7 reshape.41.qd_ref
  15.4 0.2 fusion
  15.6 0.1 copy.18
  15.7 9.4 %all-gather.3 = s32[8,2,6]{2,1,0:T(2,128)S(1)} all-gather(s32[1,2,6]{2,1,0:T(2,128)S(1)} %bitcast.30), channel_id=2, replica_groups=mesh['dp'=1,'cy'=2,'cx'=4] {'cx','cy'}, dimensions={0}, use_global_device_ids=true | all-gather | bytes 432 | tf_op jit(solution)/shard_map/all_gather | solution.py:235
  25.1 0.6 gather_fusion
  25.6 0.7 reshape.39.cnt_ref
  26.3 6.3 %copy.20 = bf16[8,256,6,2,128]{4,1,3,2,0:T(8,128)(2,1)} copy(bf16[8,256,6,2,128]{4,1,0,3,2:T(8,128)(2,1)} %bitcast.23) | data formatting | bytes 12582912 | tf_op jit(solution)/shard_map/reshape | solution.py:227
  32.6 0.0 copy-done
  32.6 0.6 pad_add_fusion.qdoc_ref
  33.2 25.1 %all-gather.7.cloned.1.call-done = bf16[16,2048,128]{2,1,0:T(8,128)(2,1)} async-done(((bf16[2,2048,128]{2,1,0:T(8,128)(2,1)}), bf16[16,2048,128]{2,1,0:T(8,128)(2,1)}) %all-gather.7.cloned.1.call-update) | async-done | bytes 8388624 | tf_op jit(solution)/shard_map/all_gather | solution.py:235
  58.3 8.2 %gather_fusion.1 = bf16[8,2,2048,128]{3,2,1,0:T(8,128)(2,1)} fusion(bf16[8,2,2048,128]{3,2,1,0:T(8,128)(2,1)} %bitcast.21, s32[1024]{0:T(1024)S(1)} %pad_clamp_fusion), kind=kCustom, calls=%fused_computation.1 | custom fusion | bytes 16777248 | tf_op jit(solution)/shard_map/gather | solution.py:238
  66.5 42.3 %all-gather.9.cloned.1.call-done = bf16[16,128,2048]{2,1,0:T(8,128)(2,1)} async-done(((bf16[2,128,2048]{2,1,0:T(8,128)(2,1)}), bf16[16,128,2048]{2,1,0:T(8,128)(2,1)}) %all-gather.9.cloned.1.call-update) | async-done | bytes 8388624 | tf_op jit(solution)/shard_map/all_gather | solution.py:235
  108.9 8.1 %gather_fusion.2 = bf16[8,2,128,2048]{3,2,1,0:T(8,128)(2,1)} fusion(bf16[8,2,128,2048]{3,2,1,0:T(8,128)(2,1)} %bitcast.22, s32[1024]{0:T(1024)S(1)} %pad_clamp_fusion), kind=kCustom, calls=%fused_computation.2 | custom fusion | bytes 16777248 | tf_op jit(solution)/shard_map/gather | solution.py:238
  116.9 194.2 %shard_map.46 = bf16[8,6,512,128]{3,2,1,0:T(8,128)(2,1)} custom-call(s32[1]{0:T(128)} %bitcast.rank_ref, s32[96]{0:T(128)} %reshape.39.cnt_ref, s32[16]{0:T(128)} %reshape.41.qd_ref, s32[8,1,512]{2,1,0:T(1,128)} %pad_add_fusion.qdoc_ref, bf16[8,6,512,128]{3,2,1,0:T(8,128)(2,1)} %bitcast.24, bf16[8,2,2048,128]{3,2,1,0:T(8,128)(2,1)} %gather_fusion.1, ...), custom_call_target="tpu_custom_call" | custom-call | flops 16000000000 | bytes 20971520 | tf_op jit(solution)/shard_map/pallas_call | solution.py:195
  311.1 6.3 %copy.23 = bf16[8,256,6,2,128]{4,1,0,3,2:T(8,128)(2,1)} copy(bf16[8,256,6,2,128]{4,1,3,2,0:T(8,128)(2,1)} %bitcast.25) | data formatting | bytes 12582912 | tf_op jit(solution)/shard_map/transpose | solution.py:240
  (3 shorter events, 0.0 us)
Async XLA Ops:
  6.5 51.8 %all-gather.7.cloned.1.call-start = ((), (), s32[]{:S(2)}) async-start(), calls=%async_computation | async-start | bytes 9437184 | tf_op jit(solution)/shard_map/all_gather | solution.py:235
  9.0 23.6 %copy-start = (s32[2048]{0:T(1024)S(1)}, s32[2048]{0:T(1024)}, u32[]{:S(2)}) copy-start(s32[2048]{0:T(1024)} %param.7) | copy-start | bytes 24580
  9.0 99.9 %all-gather.9.cloned.1.call-start = ((), (), s32[]{:S(2)}) async-start(), calls=%async_computation.1 | async-start | bytes 9437184 | tf_op jit(solution)/shard_map/all_gather | solution.py:235
Sparse Core Ops, SparseCore 0:
  9.1 49.1 all-gather.6
  60.1 48.6 all-gather.8

commit v2 on v0

v2 whole, which is shorter than its diff:
```python
import functools

import jax
import jax.numpy as jnp
from jax import lax
from jax.experimental import pallas as pl
from jax.experimental.pallas import tpu as pltpu
from jax.sharding import PartitionSpec as P

FLOOR = -1e30
MASKED = -3e38
LOG2E = 1.4426950408889634
DOCS = 6
TILE = 512
BLOCK = 512
CHUNK = 256


def fold8(x, op):
    return op(x.reshape(x.shape[0] // 8, 8, x.shape[1]), axis=0)


def attend_kernel(masks, group, first, last, rank_ref, cq_ref, cnt_ref, *rest):
    n_src = len(masks)
    q_hbm, rest = rest[:2], rest[2:]
    kv_hbm, rest = rest[:n_src], rest[n_src:]
    if not first:
        state_in, rest = rest[:2], rest[2:]
    outs, rest = rest[:2], rest[2:]
    q_ref, k_ref, v_ref, s_ref, mx_ref, ml_ref, acc_ref, o_ref, it_tile, it_sp, it_start, it_mask, it_from, sems, in_sems, out_sems = rest
    n_tiles, heads = q_ref.shape[0], q_ref.shape[1]
    piece = k_ref.shape[1] // 2
    tiles_per_piece = piece // TILE
    scale = q_ref.shape[-1] ** -0.5 * LOG2E
    rank = rank_ref[0]
    half_tiles = n_tiles // 2

    loads = [
        pltpu.make_async_copy(q_hbm[0], q_ref.at[pl.ds(0, half_tiles)], sems.at[0]),
        pltpu.make_async_copy(q_hbm[1], q_ref.at[pl.ds(half_tiles, half_tiles)], sems.at[1]),
    ]
    for src in range(n_src):
        loads.append(pltpu.make_async_copy(kv_hbm[src].at[pl.ds(0, 2 * piece)], k_ref.at[src], sems.at[2 + 2 * src]))
        loads.append(pltpu.make_async_copy(kv_hbm[src].at[pl.ds(2 * piece, 2 * piece)], v_ref.at[src], sems.at[3 + 2 * src]))
    for copy in loads:
        copy.start()

    def doc_of(tile, token):
        first_of = (tile // tiles_per_piece) * DOCS
        return sum((token >= cq_ref[first_of + d]).astype(jnp.int32) for d in range(1, DOCS))

    def list_tile(tile, count):
        it_from[tile] = count
        q_rank = jnp.where(tile < half_tiles, rank, rank ^ 2)
        q_piece = jnp.where((tile // tiles_per_piece) % 2 == 0, q_rank, 2 * group - 1 - q_rank)
        off = (tile % tiles_per_piece) * TILE
        d_first, d_last = doc_of(tile, off), doc_of(tile, off + TILE - 1)
        for sp in range(2 * n_src):
            src_rank = rank ^ masks[sp // 2]
            k_piece = src_rank if sp % 2 == 0 else 2 * group - 1 - src_rank
            lo, lo_last = cnt_ref[sp * DOCS + d_first], cnt_ref[sp * DOCS + d_last]
            diag = k_piece == q_piece
            hi = jnp.where(diag, off + TILE, piece)
            need = jnp.where(jnp.logical_and(k_piece <= q_piece, lo < hi), hi - (lo // 128) * 128, 0)
            blocks = (need + BLOCK - 1) // BLOCK
            start0 = jnp.maximum(hi - BLOCK * blocks, 0)

            def add(i, at, sp=sp, start0=start0, diag=diag, lo_last=lo_last):
                start = start0 + i * BLOCK
                it_tile[at] = tile
                it_sp[at] = sp
                it_start[at] = start
                cut = jnp.logical_or(start < lo_last, jnp.logical_and(diag, start + BLOCK > off + 1))
                it_mask[at] = jnp.where(cut, jnp.where(diag, 2, 1), 0)
                return at + 1

            count = lax.fori_loop(0, blocks, add, count)
        return count

    count = lax.fori_loop(0, n_tiles, list_tile, 0)
    it_from[n_tiles] = count

    def state_copies(tile, sem, inward):
        pairs = ((0, ml_ref), (1, acc_ref))
        if inward:
            return [pltpu.make_async_copy(state_in[i].at[tile], ref.at[tile], sem.at[i, tile]) for i, ref in pairs]
        return [pltpu.make_async_copy(ref.at[tile], outs[i].at[tile], sem.at[i, tile]) for i, ref in pairs]

    def used(tile):
        return it_from[tile + 1] > it_from[tile]

    def each_tile(fn):
        def one(tile, carry):
            if last:
                fn(tile)
            else:
                pl.when(used(tile))(lambda: fn(tile))
            return carry

        lax.fori_loop(0, n_tiles, one, 0)

    if first:
        ml_ref[:, :, 0:8, :] = jnp.zeros(ml_ref.shape[:2] + (8, TILE), jnp.float32)
        ml_ref[:, :, 8:16, :] = jnp.full(ml_ref.shape[:2] + (8, TILE), FLOOR, jnp.float32)
        acc_ref[...] = jnp.zeros_like(acc_ref)
    else:
        def fetch(tile):
            for copy in state_copies(tile, in_sems, True):
                copy.start()

        each_tile(fetch)
    for copy in loads:
        copy.wait()

    n_chunks = BLOCK // CHUNK

    def column(sp, start, j):
        return pl.ds(pl.multiple_of((sp % 2) * piece + start + j * CHUNK, 128), CHUNK)

    def values(sp, start, j):
        base = (sp % 2) * piece + start + j * CHUNK
        parts = [v_ref[sp // 2, pl.ds(pl.multiple_of(base + i * 128, 128), 128), :] for i in range(CHUNK // 128)]
        return jnp.concatenate(parts, axis=1)

    def limits(t):
        tile, sp, start = it_tile[t], it_sp[t], it_start[t]
        token = lax.broadcasted_iota(jnp.int32, (1, TILE), 1) + (tile % tiles_per_piece) * TILE
        low = jnp.full_like(token, cnt_ref[sp * DOCS])
        for d in range(1, DOCS):
            low = jnp.where(token >= cq_ref[(tile // tiles_per_piece) * DOCS + d], cnt_ref[sp * DOCS + d], low)
        return low - start, jnp.where(it_mask[t] == 2, token, piece) - start

    def score(t, h, j, bounds):
        s = lax.dot_general(
            k_ref[it_sp[t] // 2, column(it_sp[t], it_start[t], j), :], q_ref[it_tile[t], h],
            (((1,), (1,)), ((), ())), preferred_element_type=jnp.float32,
        )
        if bounds is not None:
            row = lax.broadcasted_iota(jnp.int32, s.shape, 0) + j * CHUNK
            s = jnp.where(jnp.logical_and(row >= bounds[0], row <= bounds[1]), s, MASKED)
        s_ref[h, j * CHUNK:(j + 1) * CHUNK, :] = s
        return fold8(s, jnp.max)

    @pl.when(count > 0)
    def prologue():
        bounds = limits(0)
        for h in range(heads):
            mx_ref[h] = functools.reduce(jnp.maximum, [score(0, h, j, bounds) for j in range(n_chunks)])

    def body(t, nxt, masked):
        tile, sp, start = it_tile[t], it_sp[t], it_start[t]
        bounds = limits(nxt) if masked else None
        for h in range(heads):
            m_old = ml_ref[tile, h, 8:9, :]
            m_new = jnp.maximum(m_old, jnp.max(mx_ref[h], axis=0, keepdims=True) * scale)
            rescale = jnp.exp2(m_old - m_new)
            ml_ref[tile, h, 8:9, :] = m_new
            total = ml_ref[tile, h, 0:8, :] * rescale
            prods, tops = [], []
            for j in range(n_chunks):
                p = jnp.exp2(s_ref[h, j * CHUNK:(j + 1) * CHUNK, :] * scale - m_new)
                total = total + fold8(p, jnp.sum)
                prods.append(jnp.dot(values(sp, start, j), p.astype(jnp.bfloat16), preferred_element_type=jnp.float32))
                tops.append(score(nxt, h, j, bounds))
            mx_ref[h] = functools.reduce(jnp.maximum, tops)
            ml_ref[tile, h, 0:8, :] = total
            acc_ref[tile, h] = acc_ref[tile, h] * rescale + functools.reduce(jnp.add, prods)

    def step(t, carry):
        nxt = jnp.minimum(t + 1, count - 1)
        masked = it_mask[nxt] > 0
        pl.when(masked)(lambda: body(t, nxt, True))
        pl.when(jnp.logical_not(masked))(lambda: body(t, nxt, False))
        return carry

    def out_copy(tile, dst, base):
        return pltpu.make_async_copy(o_ref.at[tile], dst.at[tile - base], out_sems.at[0, tile])

    def send_out(tile, act):
        pl.when(tile < half_tiles)(lambda: act(out_copy(tile, outs[0], 0)))
        pl.when(tile >= half_tiles)(lambda: act(out_copy(tile, outs[1], half_tiles)))

    def run_tile(tile):
        if not first:
            for copy in state_copies(tile, in_sems, True):
                copy.wait()
        lax.fori_loop(it_from[tile], it_from[tile + 1], step, 0)
        if last:
            for h in range(heads):
                denom = jnp.sum(ml_ref[tile, h, 0:8, :], axis=0, keepdims=True)
                o_ref[tile, h] = (acc_ref[tile, h] / denom).T.astype(o_ref.dtype)
            send_out(tile, lambda copy: copy.start())
        else:
            for copy in state_copies(tile, out_sems, False):
                copy.start()

    each_tile(run_tile)

    def settle(tile):
        if last:
            send_out(tile, lambda copy: copy.wait())
        else:
            for copy in state_copies(tile, out_sems, False):
                copy.wait()

    each_tile(settle)


def attend(masks, group, rank, cq, cnt, q, kvs, state, last):
    half_tiles, heads, _, dim = q[1].shape
    n_tiles, n_src = 2 * half_tiles, len(masks)
    first = state is None
    stat = [(n_tiles, heads, 16, TILE), (n_tiles, heads, dim, TILE)]
    if last:
        out_shape = [jax.ShapeDtypeStruct(q[1].shape, jnp.bfloat16)] * 2
    else:
        out_shape = [jax.ShapeDtypeStruct(shape, jnp.float32) for shape in stat]
    state = () if first else tuple(state)
    any_spec = pl.BlockSpec(memory_space=pl.ANY)
    smem = pl.BlockSpec(memory_space=pltpu.SMEM)
    rows = 2 * (kvs[0].shape[0] // 4 // 128 * 128)
    items = 2 * n_tiles * 2 * n_src
    n_front = 3 + 2 + n_src
    aliases = {n_front + i: i for i in range(2)} if not first and not last else {}
    return pl.pallas_call(
        functools.partial(attend_kernel, masks, group, first, last),
        out_shape=out_shape,
        in_specs=[smem] * 3 + [any_spec] * (2 + n_src + len(state)),
        out_specs=[any_spec] * 2,
        scratch_shapes=[
            pltpu.VMEM((n_tiles,) + q[1].shape[1:], jnp.bfloat16),
            *[pltpu.VMEM((n_src, rows, dim), jnp.bfloat16)] * 2,
            pltpu.VMEM((heads, BLOCK, TILE), jnp.float32),
            pltpu.VMEM((heads, 8, TILE), jnp.float32),
            *[pltpu.VMEM(shape, jnp.float32) for shape in stat],
            pltpu.VMEM(((n_tiles,) + q[1].shape[1:]) if last else (8, 128), jnp.bfloat16),
            *[pltpu.SMEM((items,), jnp.int32)] * 4,
            pltpu.SMEM((n_tiles + 1,), jnp.int32),
            pltpu.SemaphoreType.DMA((2 + 2 * n_src,)),
            pltpu.SemaphoreType.DMA((2, n_tiles)),
            pltpu.SemaphoreType.DMA((2, n_tiles)),
        ],
        input_output_aliases=aliases,
        compiler_params=pltpu.CompilerParams(vmem_limit_bytes=60 * 1024 * 1024),
        cost_estimate=pl.CostEstimate(flops=n_src * 10**10, bytes_accessed=20 << 20, transcendentals=0),
    )(rank, cq, cnt, *q, *kvs, *state)


def solution(mesh):
    size_cx, size_cy = mesh.shape['cx'], mesh.shape['cy']
    group = size_cx * size_cy
    seq_spec = P(('dp', 'cx', 'cy'), None, None)

    def swap(array, mask):
        pairs = []
        for y in range(size_cy):
            for x in range(size_cx):
                other = (x * size_cy + y) ^ mask
                pairs.append((y * size_cx + x, (other % size_cy) * size_cx + other // size_cy))
        return lax.ppermute(array, ('cy', 'cx'), pairs)

    def per_device(q_loc, k_loc, v_loc, doc_loc):
        tok, heads, dim = q_loc.shape
        kv_heads = k_loc.shape[1]
        per_kv = heads // kv_heads
        piece, half_tiles = tok // 2, tok // TILE
        rank = lax.axis_index('cx') * size_cy + lax.axis_index('cy')
        core = (rank // 2) % 2

        def pick(array, index):
            return lax.dynamic_index_in_dim(array, index, 0, keepdims=False)

        cnt = jnp.sum(doc_loc.reshape(2, 1, piece) < jnp.arange(DOCS)[None, :, None], axis=-1).astype(jnp.int32).reshape(-1)
        digits = jnp.stack([cnt // 64, cnt % 64]).astype(jnp.bfloat16)
        digits = jnp.pad(digits, ((0, 14), (0, dim - digits.shape[1])))
        k_heads = k_loc.transpose(1, 0, 2)
        v_heads = v_loc.reshape(tok // 128, 128, kv_heads, dim).transpose(2, 0, 3, 1).reshape(kv_heads, tok, dim)
        kv = jnp.concatenate([k_heads, v_heads, jnp.broadcast_to(digits, (kv_heads,) + digits.shape)], axis=1)
        kv_mine, kv_other = pick(kv, core), pick(kv, 1 - core)

        def tile_heads(index):
            half = lax.dynamic_index_in_dim(q_loc.reshape(tok, kv_heads, per_kv, dim), index, 1, keepdims=False)
            return half.reshape(half_tiles, TILE, per_kv, dim).transpose(0, 2, 1, 3)

        q = (tile_heads(core), swap(tile_heads(1 - core), 2))
        kvs = {0: kv_mine}

        def fetch(masks, mine, other):
            for mask in masks:
                kvs[mask] = swap(other if mask & 2 else mine, mask)

        fetch((2, 4, 6, 1, 3), kv_mine, kv_other)

        def counts(masks):
            rows = jnp.stack([kvs[i][2 * tok:2 * tok + 2, :2 * DOCS] for i in masks]).astype(jnp.float32)
            return (rows[:, 0] * 64 + rows[:, 1]).astype(jnp.int32).reshape(-1)

        cq = counts((0, 2))

        def stage(masks, state, last):
            return attend(masks, group, rank[None], cq, counts(masks), q, [kvs[i] for i in masks], state, last)

        state = stage((0, 2), None, False)
        near, far = (4, 6, 1, 3), (5, 7)
        state, held, late = lax.optimization_barrier((state, [kvs[i] for i in near], (kv_mine, kv_other)))
        kvs.update(zip(near, held))
        fetch(far, *late)
        state = stage(near, state, False)
        state, held = lax.optimization_barrier((state, [kvs[i] for i in far]))
        kvs.update(zip(far, held))
        o_mine, o_other = stage(far, state, True)
        o_back = swap(o_other, 2)
        even = core == 0
        out = jnp.stack([jnp.where(even, o_mine, o_back), jnp.where(even, o_back, o_mine)])
        return out.transpose(1, 3, 0, 2, 4).reshape(tok, heads, dim)

    return jax.shard_map(per_device, mesh=mesh, in_specs=(seq_spec, seq_spec, seq_spec, P(('dp', 'cx', 'cy'))), out_specs=seq_spec, check_vma=False)
```

time: 1490 us -> 209 us (0.14)
  the two profiles are of different devices: /device:TPU:7 before, /device:TPU:6 now
where the time goes in v2:
time: 209 us; the launch traced here: 208 us
  Pallas kernels  167 us (80%)
  local copies, waits for them, and re-layouts  22.4 us (11%)
  starting transfers between devices  7.24 us (3%)
  waiting for transfers between devices  5.52 us (3%)
  other arithmetic  4.88 us (2%)
    pallas_call x3, Pallas kernels, attend(): pl.pallas_call(functools.partial(attend_kernel, masks, group, first, last...  167 us
    ppermute x9, starting transfers between devices, swap(): return lax.ppermute(array, ('cy', 'cx'), pairs)  7.24 us
    ppermute x9, waiting for transfers between devices, swap(): return lax.ppermute(array, ('cy', 'cx'), pairs)  5.52 us
  transfers between devices with their start and end apart: 9, of which 1 were waited for; matrix products, arithmetic and copies ran while one was open for 6% of the time, Pallas kernels for 62%

profile of v2, /device:TPU:6, one launch (start us, length us, event | category | flops | bytes accessed | tf_op | source)
XLA Modules:
  0.0 207.6 jit_solution(11521325470980671235)
XLA Ops:
  0.0 3.2 %constant_dynamic-slice_fusion = (bf16[2048,1,6,128]{3,0,2,1:T(8,128)(2,1)S(1)}, bf16[2048,1,6,128]{3,0,2,1:T(8,128)(2,1)S(1)}) fusion(bf16[2048,2,6,128]{3,0,2,1:T(8,128)(2,1)} %bitcast.46, s32[]{:T(128)S(6)} %select_n.64, s32[]{:T(128)S(6)} %select_n.63), kind=kLoop, calls=%fused_computation.39 | loop fusion | bytes 12582920 | tf_op jit(solution)/shard_map/jit(dynamic_index_in_dim)/dynamic_slice | solution.py:282
  3.3 1.8 copy.22
  5.1 0.2 fusion
  5.3 0.1 copy.15
  5.4 0.1 reshape.152
  5.5 2.4 %copy.24 = bf16[2048,2,128]{2,0,1:T(8,128)(2,1)} copy(bf16[2048,2,128]{2,1,0:T(2,128)(2,1)} %param.5) | data formatting | bytes 2097152 | tf_op args[1]
  7.9 3.7 %copy.14 = bf16[16,128,2,128]{1,3,0,2:T(8,128)(2,1)} copy(bf16[16,128,2,128]{3,2,1,0:T(2,128)(2,1)} %bitcast.52) | data formatting | bytes 2097152 | tf_op jit(solution)/shard_map/reshape | solution.py:277
  11.6 1.7 pad_maximum_fusion
  13.2 1.6 dynamic-slice_bitcast_fusion.1
  14.8 0.4 collective-permute-start
  15.2 0.2 collective-permute-start.5
  15.4 0.0 collective-permute-start.3
  15.5 2.0 collective-permute-start.4
  17.5 1.9 copy.23
  19.3 0.7 slice_bitcast_fusion.1
  20.0 1.5 collective-permute-start.2
  21.6 0.6 convert_element_type.41.cq_ref.cnt_ref
  22.1 53.3 %shard_map.46 = (f32[8,6,16,512]{3,2,1,0:T(8,128)}, f32[8,6,128,512]{3,2,1,0:T(8,128)}) custom-call(s32[1]{0:T(128)} %bitcast.rank_ref, s32[24]{0:T(128)} %convert_element_type.41.cq_ref.cnt_ref, s32[24]{0:T(128)} %convert_element_type.41.cq_ref.cnt_ref, bf16[4,6,512,128]{3,2,1,0:T(8,128)(2,1)} %bitcast.49, ...), custom_call_target="tpu_custom_call" | custom-call | flops 20000000000 | bytes 20971520 | tf_op jit(solution)/shard_map/pallas_call | solution.py:225
  75.5 0.7 slice_bitcast_fusion.6
  76.2 0.7 slice_bitcast_fusion.4
  76.9 0.6 convert_element_type.44.cnt_ref
  77.5 1.8 collective-permute-start.7
  79.3 76.5 %shard_map.47 = (f32[8,6,16,512]{3,2,1,0:T(8,128)}, f32[8,6,128,512]{3,2,1,0:T(8,128)}) custom-call(s32[1]{0:T(128)} %bitcast.rank_ref, s32[24]{0:T(128)} %convert_element_type.41.cq_ref.cnt_ref, s32[48]{0:T(128)} %convert_element_type.44.cnt_ref, bf16[4,6,512,128]{3,2,1,0:T(8,128)(2,1)} %bitcast.50, ...), custom_call_target="tpu_custom_call", output_to_operand_aliasing={{0}: (9, {}), {1}: (10, {})} | custom-call | flops 40000000000 | bytes 20971520 | tf_op jit(solution)/shard_map/pallas_call | solution.py:225
  155.9 0.7 convert_element_type.47.cnt_ref
  156.6 0.1 copy-done.3
  156.8 0.4 copy-done.4
  157.2 37.7 %shard_map.48 = (bf16[4,6,512,128]{3,2,1,0:T(8,128)(2,1)}, bf16[4,6,512,128]{3,2,1,0:T(8,128)(2,1)}) custom-call(s32[1]{0:T(128)} %bitcast.rank_ref, s32[24]{0:T(128)} %convert_element_type.41.cq_ref.cnt_ref, s32[24]{0:T(128)} %convert_element_type.47.cnt_ref, bf16[4,6,512,128]{3,2,1,0:T(8,128)(2,1)} %bitcast.51, ...), custom_call_target="tpu_custom_call" | custom-call | flops 20000000000 | bytes 20971520 | tf_op jit(solution)/shard_map/pallas_call | solution.py:225
  194.9 1.3 collective-permute-start.8
  196.1 5.5 %collective-permute-done.8 = bf16[4,6,512,128]{3,2,1,0:T(8,128)(2,1)S(1)} collective-permute-done((bf16[4,6,512,128]{3,2,1,0:T(8,128)(2,1)}, bf16[4,6,512,128]{3,2,1,0:T(8,128)(2,1)S(1)}, u32[]{:S(2)}, u32[]{:S(2)}) %collective-permute-start.8) | collective-permute-done | bytes 3145760 | tf_op jit(solution)/shard_map/ppermute | solution.py:260
  201.6 2.3 %select_bitcast_fusion.1 = (bf16[1,4,6,512,128]{4,3,2,1,0:T(8,128)(2,1)S(1)}, bf16[1,4,6,512,128]{4,3,2,1,0:T(8,128)(2,1)S(1)}) fusion(bf16[4,6,512,128]{3,2,1,0:T(8,128)(2,1)} %get-tuple-element.39, bf16[4,6,512,128]{3,2,1,0:T(8,128)(2,1)S(1)} %collective-permute-done.8, pred[]{:T(512)S(6)} %eq.7), kind=kLoop, calls=%fused_computation.4 | loop fusion | flops 3145728 | bytes 12582913 | tf_op jit(solution)/shard_map/stack | solution.py:314
  203.9 0.6 maximum_bitcast_fusion
  204.5 3.1 %copy.18 = bf16[4,512,2,6,128]{4,1,0,3,2:T(8,128)(2,1)} copy(bf16[4,512,2,6,128]{4,1,3,0,2:T(8,128)(2,1)S(1)} %maximum_bitcast_fusion) | data formatting | bytes 12582912 | tf_op jit(solution)/shard_map/transpose | solution.py:315
  (31 shorter events, 0.2 us)
Async XLA Ops:
  3.3 1.9 copy-start
  5.1 17.0 %collective-permute-start.1 = (bf16[4,6,512,128]{3,2,1,0:T(8,128)(2,1)}, bf16[4,6,512,128]{3,2,1,0:T(8,128)(2,1)}, u32[]{:S(2)}, u32[]{:S(2)}) collective-permute-start(bf16[4,6,512,128]{3,2,1,0:T(8,128)(2,1)} %bitcast.41), channel_id=1, source_target_pairs={{0,1},{1,0},{2,3},{3,2},{4,5},{5,4},{6,7},{7,6}} | collective-permute-start | bytes 9437192 | tf_op jit(solution)/shard_map/ppermute | solution.py:260
  14.8 5.2 %collective-permute-start = (bf16[4112,128]{1,0:T(8,128)(2,1)}, bf16[4112,128]{1,0:T(8,128)(2,1)S(1)}, u32[]{:S(2)}, u32[]{:S(2)}) collective-permute-start(bf16[4112,128]{1,0:T(8,128)(2,1)} %get-tuple-element.34), channel_id=1, source_target_pairs={{0,1},{1,0},{2,3},{3,2},{4,5},{5,4},{6,7},{7,6}} | collective-permute-start | bytes 3158024 | tf_op jit(solution)/shard_map/ppermute | solution.py:260
  15.2 60.2 %collective-permute-start.5 = (bf16[4112,128]{1,0:T(8,128)(2,1)}, bf16[4112,128]{1,0:T(8,128)(2,1)}, u32[]{:S(2)}, u32[]{:S(2)}) collective-permute-start(bf16[4112,128]{1,0:T(8,128)(2,1)} %get-tuple-element.34), channel_id=1, source_target_pairs={{0,5},{1,4},{2,7},{3,6},{4,1},{5,0},{6,3},{7,2}} | collective-permute-start | bytes 3158024 | tf_op jit(solution)/shard_map/ppermute | solution.py:260
  15.4 60.0 %collective-permute-start.3 = (bf16[4112,128]{1,0:T(8,128)(2,1)}, bf16[4112,128]{1,0:T(8,128)(2,1)}, u32[]{:S(2)}, u32[]{:S(2)}) collective-permute-start(bf16[4112,128]{1,0:T(8,128)(2,1)} %get-tuple-element.34), channel_id=1, source_target_pairs={{0,3},{1,2},{2,1},{3,0},{4,7},{5,6},{6,5},{7,4}} | collective-permute-start | bytes 3158024 | tf_op jit(solution)/shard_map/ppermute | solution.py:260
  15.5 60.0 %collective-permute-start.4 = (bf16[4112,128]{1,0:T(8,128)(2,1)}, bf16[4112,128]{1,0:T(8,128)(2,1)}, u32[]{:S(2)}, u32[]{:S(2)}) collective-permute-start(bf16[4112,128]{1,0:T(8,128)(2,1)} %get-tuple-element.33.rest_2_), channel_id=1, source_target_pairs={{0,4},{1,5},{2,6},{3,7},{4,0},{5,1},{6,2},{7,3}} | collective-permute-start | bytes 3158024 | tf_op jit(solution)/shard_map/ppermute | solution.py:260
  20.0 1.5 copy-start.2
  20.0 55.4 %collective-permute-start.2 = (bf16[4112,128]{1,0:T(8,128)(2,1)}, bf16[4112,128]{1,0:T(8,128)(2,1)S(1)}, u32[]{:S(2)}, u32[]{:S(2)}) collective-permute-start(bf16[4112,128]{1,0:T(8,128)(2,1)} %get-tuple-element.33.rest_2_), channel_id=1, source_target_pairs={{0,2},{1,3},{2,0},{3,1},{4,6},{5,7},{6,4},{7,5}} | collective-permute-start | bytes 3158024 | tf_op jit(solution)/shard_map/ppermute | solution.py:260
  75.5 3.9 %copy-start.1 = (bf16[4112,128]{1,0:T(8,128)(2,1)}, bf16[4112,128]{1,0:T(8,128)(2,1)S(1)}, u32[]{:S(2)}) copy-start(bf16[4112,128]{1,0:T(8,128)(2,1)S(1)} %collective-permute-done.2.rest_2_) | copy-start | bytes 3158020
  77.5 78.3 %collective-permute-start.6 = (bf16[4112,128]{1,0:T(8,128)(2,1)}, bf16[4112,128]{1,0:T(8,128)(2,1)S(1)}, u32[]{:S(2)}, u32[]{:S(2)}) collective-permute-start(bf16[4112,128]{1,0:T(8,128)(2,1)} %get-tuple-element.33.rest_2_), channel_id=1, source_target_pairs={{0,6},{1,7},{2,4},{3,5},{4,2},{5,3},{6,0},{7,1}} | collective-permute-start | bytes 3158024 | tf_op jit(solution)/shard_map/ppermute | solution.py:260
  77.5 78.3 %collective-permute-start.7 = (bf16[4112,128]{1,0:T(8,128)(2,1)}, bf16[4112,128]{1,0:T(8,128)(2,1)S(1)}, u32[]{:S(2)}, u32[]{:S(2)}) collective-permute-start(bf16[4112,128]{1,0:T(8,128)(2,1)} %get-tuple-element.34), channel_id=1, source_target_pairs={{0,7},{1,6},{2,5},{3,4},{4,3},{5,2},{6,1},{7,0}} | collective-permute-start | bytes 3158024 | tf_op jit(solution)/shard_map/ppermute | solution.py:260
  155.8 1.0 copy-start.3
  155.8 1.4 copy-start.4
  194.9 6.8 %collective-permute-start.8 = (bf16[4,6,512,128]{3,2,1,0:T(8,128)(2,1)}, bf16[4,6,512,128]{3,2,1,0:T(8,128)(2,1)S(1)}, u32[]{:S(2)}, u32[]{:S(2)}) collective-permute-start(bf16[4,6,512,128]{3,2,1,0:T(8,128)(2,1)} %get-tuple-element.40), channel_id=1, source_target_pairs={{0,1},{1,0},{2,3},{3,2},{4,5},{5,4},{6,7},{7,6}} | collective-permute-start | bytes 9437192 | tf_op jit(solution)/shard_map/ppermute | solution.py:260

commit v3 on v2

--- a/solution.py
+++ b/solution.py
@@ -27,7 +27,7 @@
     if not first:
         state_in, rest = rest[:2], rest[2:]
     outs, rest = rest[:2], rest[2:]
-    q_ref, k_ref, v_ref, s_ref, mx_ref, ml_ref, acc_ref, o_ref, it_tile, it_sp, it_start, it_mask, it_from, sems, in_sems, out_sems = rest
+    q_ref, k_ref, v_ref, s_ref, cap_ref, mx_ref, ml_ref, acc_ref, o_ref, it_tile, it_sp, it_start, it_mask, it_from, sems, in_sems, out_sems = rest
     n_tiles, heads = q_ref.shape[0], q_ref.shape[1]
     piece = k_ref.shape[1] // 2
     tiles_per_piece = piece // TILE
@@ -122,34 +122,39 @@
         parts = [v_ref[sp // 2, pl.ds(pl.multiple_of(base + i * 128, 128), 128), :] for i in range(CHUNK // 128)]
         return jnp.concatenate(parts, axis=1)
 
-    def limits(t):
+    def set_caps(t):
         tile, sp, start = it_tile[t], it_sp[t], it_start[t]
         token = lax.broadcasted_iota(jnp.int32, (1, TILE), 1) + (tile % tiles_per_piece) * TILE
         low = jnp.full_like(token, cnt_ref[sp * DOCS])
         for d in range(1, DOCS):
             low = jnp.where(token >= cq_ref[(tile // tiles_per_piece) * DOCS + d], cnt_ref[sp * DOCS + d], low)
-        return low - start, jnp.where(it_mask[t] == 2, token, piece) - start
-
-    def score(t, h, j, bounds):
+        low = low - start
+        high = jnp.where(it_mask[t] == 2, token, piece) - start
+        for j in range(n_chunks):
+            row = lax.broadcasted_iota(jnp.int32, (CHUNK, TILE), 0) + j * CHUNK
+            keep = jnp.logical_and(row >= low, row <= high)
+            cap_ref[j * CHUNK:(j + 1) * CHUNK, :] = jnp.where(keep, jnp.inf, MASKED)
+
+    def score(t, h, j, masked):
         s = lax.dot_general(
             k_ref[it_sp[t] // 2, column(it_sp[t], it_start[t], j), :], q_ref[it_tile[t], h],
             (((1,), (1,)), ((), ())), preferred_element_type=jnp.float32,
         )
-        if bounds is not None:
-            row = lax.broadcasted_iota(jnp.int32, s.shape, 0) + j * CHUNK
-            s = jnp.where(jnp.logical_and(row >= bounds[0], row <= bounds[1]), s, MASKED)
+        if masked:
+            s = jnp.minimum(s, cap_ref[j * CHUNK:(j + 1) * CHUNK, :])
         s_ref[h, j * CHUNK:(j + 1) * CHUNK, :] = s
         return fold8(s, jnp.max)
 
     @pl.when(count > 0)
     def prologue():
-        bounds = limits(0)
+        set_caps(0)
         for h in range(heads):
-            mx_ref[h] = functools.reduce(jnp.maximum, [score(0, h, j, bounds) for j in range(n_chunks)])
+            mx_ref[h] = functools.reduce(jnp.maximum, [score(0, h, j, True) for j in range(n_chunks)])
 
     def body(t, nxt, masked):
         tile, sp, start = it_tile[t], it_sp[t], it_start[t]
-        bounds = limits(nxt) if masked else None
+        if masked:
+            set_caps(nxt)
         for h in range(heads):
             m_old = ml_ref[tile, h, 8:9, :]
             m_new = jnp.maximum(m_old, jnp.max(mx_ref[h], axis=0, keepdims=True) * scale)
@@ -161,7 +166,7 @@
                 p = jnp.exp2(s_ref[h, j * CHUNK:(j + 1) * CHUNK, :] * scale - m_new)
                 total = total + fold8(p, jnp.sum)
                 prods.append(jnp.dot(values(sp, start, j), p.astype(jnp.bfloat16), preferred_element_type=jnp.float32))
-                tops.append(score(nxt, h, j, bounds))
+                tops.append(score(nxt, h, j, masked))
             mx_ref[h] = functools.reduce(jnp.maximum, tops)
             ml_ref[tile, h, 0:8, :] = total
             acc_ref[tile, h] = acc_ref[tile, h] * rescale + functools.reduce(jnp.add, prods)
@@ -187,8 +192,8 @@
         lax.fori_loop(it_from[tile], it_from[tile + 1], step, 0)
         if last:
             for h in range(heads):
-                denom = jnp.sum(ml_ref[tile, h, 0:8, :], axis=0, keepdims=True)
-                o_ref[tile, h] = (acc_ref[tile, h] / denom).T.astype(o_ref.dtype)
+                inverse = 1.0 / jnp.sum(ml_ref[tile, h, 0:8, :], axis=0, keepdims=True)
+                o_ref[tile, h] = (acc_ref[tile, h] * inverse).T.astype(o_ref.dtype)
             send_out(tile, lambda copy: copy.start())
         else:
             for copy in state_copies(tile, out_sems, False):
@@ -231,6 +236,7 @@
             pltpu.VMEM((n_tiles,) + q[1].shape[1:], jnp.bfloat16),
             *[pltpu.VMEM((n_src, rows, dim), jnp.bfloat16)] * 2,
             pltpu.VMEM((heads, BLOCK, TILE), jnp.float32),
+            pltpu.VMEM((BLOCK, TILE), jnp.float32),
             pltpu.VMEM((heads, 8, TILE), jnp.float32),
             *[pltpu.VMEM(shape, jnp.float32) for shape in stat],
             pltpu.VMEM(((n_tiles,) + q[1].shape[1:]) if last else (8, 128), jnp.bfloat16),

time: 209 us -> 201 us (0.962)
  Pallas kernels: 167 us -> 160 us
    pallas_call x3, Pallas kernels: 167 us -> 160 us  [attend(): pl.pallas_call(functools.partial(attend_kernel, masks, group, first, last...]
where the time goes in v3:
time: 201 us; the launch traced here: 200 us
  Pallas kernels  160 us (80%)
  local copies, waits for them, and re-layouts  22.4 us (11%)
  starting transfers between devices  7.25 us (4%)
  waiting for transfers between devices  5.52 us (3%)
  other arithmetic  4.88 us (2%)
    pallas_call x3, Pallas kernels, attend(): pl.pallas_call(functools.partial(attend_kernel, masks, group, first, last...  160 us
    ppermute x9, starting transfers between devices, swap(): return lax.ppermute(array, ('cy', 'cx'), pairs)  7.25 us
    ppermute x9, waiting for transfers between devices, swap(): return lax.ppermute(array, ('cy', 'cx'), pairs)  5.52 us
  transfers between devices with their start and end apart: 9, of which 1 were waited for; matrix products, arithmetic and copies ran while one was open for 6% of the time, Pallas kernels for 62%

profile of v3, /device:TPU:6, one launch (start us, length us, event | category | flops | bytes accessed | tf_op | source)
XLA Modules:
  0.0 200.0 jit_solution(2728419632854503951)
XLA Ops:
  0.0 3.2 %constant_dynamic-slice_fusion = (bf16[2048,1,6,128]{3,0,2,1:T(8,128)(2,1)S(1)}, bf16[2048,1,6,128]{3,0,2,1:T(8,128)(2,1)S(1)}) fusion(bf16[2048,2,6,128]{3,0,2,1:T(8,128)(2,1)} %bitcast.46, s32[]{:T(128)S(6)} %select_n.64, s32[]{:T(128)S(6)} %select_n.63), kind=kLoop, calls=%fused_computation.39 | loop fusion | bytes 12582920 | tf_op jit(solution)/shard_map/jit(dynamic_index_in_dim)/dynamic_slice | solution.py:288
  3.3 1.8 copy.22
  5.1 0.2 fusion
  5.3 0.1 copy.15
  5.4 0.1 reshape.152
  5.5 2.4 %copy.24 = bf16[2048,2,128]{2,0,1:T(8,128)(2,1)} copy(bf16[2048,2,128]{2,1,0:T(2,128)(2,1)} %param.5) | data formatting | bytes 2097152 | tf_op args[1]
  7.9 3.7 %copy.14 = bf16[16,128,2,128]{1,3,0,2:T(8,128)(2,1)} copy(bf16[16,128,2,128]{3,2,1,0:T(2,128)(2,1)} %bitcast.52) | data formatting | bytes 2097152 | tf_op jit(solution)/shard_map/reshape | solution.py:283
  11.6 1.7 pad_maximum_fusion
  13.2 1.6 dynamic-slice_bitcast_fusion.1
  14.8 0.4 collective-permute-start
  15.2 0.2 collective-permute-start.5
  15.4 0.0 collective-permute-start.3
  15.5 2.0 %collective-permute-start.4 = (bf16[4112,128]{1,0:T(8,128)(2,1)}, bf16[4112,128]{1,0:T(8,128)(2,1)}, u32[]{:S(2)}, u32[]{:S(2)}) collective-permute-start(bf16[4112,128]{1,0:T(8,128)(2,1)} %get-tuple-element.33.rest_2_), channel_id=1, source_target_pairs={{0,4},{1,5},{2,6},{3,7},{4,0},{5,1},{6,2},{7,3}} | collective-permute-start | bytes 3158024 | tf_op jit(solution)/shard_map/ppermute | solution.py:266
  17.5 1.9 copy.23
  19.3 0.7 slice_bitcast_fusion.1
  20.0 1.5 collective-permute-start.2
  21.6 0.6 convert_element_type.41.cq_ref.cnt_ref
  22.1 49.6 %shard_map.46 = (f32[8,6,16,512]{3,2,1,0:T(8,128)}, f32[8,6,128,512]{3,2,1,0:T(8,128)}) custom-call(s32[1]{0:T(128)} %bitcast.rank_ref, s32[24]{0:T(128)} %convert_element_type.41.cq_ref.cnt_ref, s32[24]{0:T(128)} %convert_element_type.41.cq_ref.cnt_ref, bf16[4,6,512,128]{3,2,1,0:T(8,128)(2,1)} %bitcast.49, ...), custom_call_target="tpu_custom_call" | custom-call | flops 20000000000 | bytes 20971520 | tf_op jit(solution)/shard_map/pallas_call | solution.py:230
  71.8 0.7 slice_bitcast_fusion.6
  72.5 0.7 slice_bitcast_fusion.4
  73.2 0.6 convert_element_type.44.cnt_ref
  73.8 1.8 collective-permute-start.7
  75.7 74.3 %shard_map.47 = (f32[8,6,16,512]{3,2,1,0:T(8,128)}, f32[8,6,128,512]{3,2,1,0:T(8,128)}) custom-call(s32[1]{0:T(128)} %bitcast.rank_ref, s32[24]{0:T(128)} %convert_element_type.41.cq_ref.cnt_ref, s32[48]{0:T(128)} %convert_element_type.44.cnt_ref, bf16[4,6,512,128]{3,2,1,0:T(8,128)(2,1)} %bitcast.50, ...), custom_call_target="tpu_custom_call", output_to_operand_aliasing={{0}: (9, {}), {1}: (10, {})} | custom-call | flops 40000000000 | bytes 20971520 | tf_op jit(solution)/shard_map/pallas_call | solution.py:230
  150.0 0.7 convert_element_type.47.cnt_ref
  150.8 0.1 copy-done.3
  150.9 0.4 copy-done.4
  151.3 35.9 %shard_map.48 = (bf16[4,6,512,128]{3,2,1,0:T(8,128)(2,1)}, bf16[4,6,512,128]{3,2,1,0:T(8,128)(2,1)}) custom-call(s32[1]{0:T(128)} %bitcast.rank_ref, s32[24]{0:T(128)} %convert_element_type.41.cq_ref.cnt_ref, s32[24]{0:T(128)} %convert_element_type.47.cnt_ref, bf16[4,6,512,128]{3,2,1,0:T(8,128)(2,1)} %bitcast.51, ...), custom_call_target="tpu_custom_call" | custom-call | flops 20000000000 | bytes 20971520 | tf_op jit(solution)/shard_map/pallas_call | solution.py:230
  187.3 1.3 collective-permute-start.8
  188.5 5.5 %collective-permute-done.8 = bf16[4,6,512,128]{3,2,1,0:T(8,128)(2,1)S(1)} collective-permute-done((bf16[4,6,512,128]{3,2,1,0:T(8,128)(2,1)}, bf16[4,6,512,128]{3,2,1,0:T(8,128)(2,1)S(1)}, u32[]{:S(2)}, u32[]{:S(2)}) %collective-permute-start.8) | collective-permute-done | bytes 3145760 | tf_op jit(solution)/shard_map/ppermute | solution.py:266
  194.0 2.3 %select_bitcast_fusion.1 = (bf16[1,4,6,512,128]{4,3,2,1,0:T(8,128)(2,1)S(1)}, bf16[1,4,6,512,128]{4,3,2,1,0:T(8,128)(2,1)S(1)}) fusion(bf16[4,6,512,128]{3,2,1,0:T(8,128)(2,1)} %get-tuple-element.39, bf16[4,6,512,128]{3,2,1,0:T(8,128)(2,1)S(1)} %collective-permute-done.8, pred[]{:T(512)S(6)} %eq.7), kind=kLoop, calls=%fused_computation.4 | loop fusion | flops 3145728 | bytes 12582913 | tf_op jit(solution)/shard_map/stack | solution.py:320
  196.3 0.6 maximum_bitcast_fusion
  196.9 3.1 %copy.18 = bf16[4,512,2,6,128]{4,1,0,3,2:T(8,128)(2,1)} copy(bf16[4,512,2,6,128]{4,1,3,0,2:T(8,128)(2,1)S(1)} %maximum_bitcast_fusion) | data formatting | bytes 12582912 | tf_op jit(solution)/shard_map/transpose | solution.py:321
  (31 shorter events, 0.2 us)
Async XLA Ops:
  3.3 1.9 copy-start
  5.1 17.0 %collective-permute-start.1 = (bf16[4,6,512,128]{3,2,1,0:T(8,128)(2,1)}, bf16[4,6,512,128]{3,2,1,0:T(8,128)(2,1)}, u32[]{:S(2)}, u32[]{:S(2)}) collective-permute-start(bf16[4,6,512,128]{3,2,1,0:T(8,128)(2,1)} %bitcast.41), channel_id=1, source_target_pairs={{0,1},{1,0},{2,3},{3,2},{4,5},{5,4},{6,7},{7,6}} | collective-permute-start | bytes 9437192 | tf_op jit(solution)/shard_map/ppermute | solution.py:266
  14.8 5.2 %collective-permute-start = (bf16[4112,128]{1,0:T(8,128)(2,1)}, bf16[4112,128]{1,0:T(8,128)(2,1)S(1)}, u32[]{:S(2)}, u32[]{:S(2)}) collective-permute-start(bf16[4112,128]{1,0:T(8,128)(2,1)} %get-tuple-element.34), channel_id=1, source_target_pairs={{0,1},{1,0},{2,3},{3,2},{4,5},{5,4},{6,7},{7,6}} | collective-permute-start | bytes 3158024 | tf_op jit(solution)/shard_map/ppermute | solution.py:266
  15.2 56.6 %collective-permute-start.5 = (bf16[4112,128]{1,0:T(8,128)(2,1)}, bf16[4112,128]{1,0:T(8,128)(2,1)}, u32[]{:S(2)}, u32[]{:S(2)}) collective-permute-start(bf16[4112,128]{1,0:T(8,128)(2,1)} %get-tuple-element.34), channel_id=1, source_target_pairs={{0,5},{1,4},{2,7},{3,6},{4,1},{5,0},{6,3},{7,2}} | collective-permute-start | bytes 3158024 | tf_op jit(solution)/shard_map/ppermute | solution.py:266
  15.4 56.3 %collective-permute-start.3 = (bf16[4112,128]{1,0:T(8,128)(2,1)}, bf16[4112,128]{1,0:T(8,128)(2,1)}, u32[]{:S(2)}, u32[]{:S(2)}) collective-permute-start(bf16[4112,128]{1,0:T(8,128)(2,1)} %get-tuple-element.34), channel_id=1, source_target_pairs={{0,3},{1,2},{2,1},{3,0},{4,7},{5,6},{6,5},{7,4}} | collective-permute-start | bytes 3158024 | tf_op jit(solution)/shard_map/ppermute | solution.py:266
  15.5 56.3 %collective-permute-start.4 = (bf16[4112,128]{1,0:T(8,128)(2,1)}, bf16[4112,128]{1,0:T(8,128)(2,1)}, u32[]{:S(2)}, u32[]{:S(2)}) collective-permute-start(bf16[4112,128]{1,0:T(8,128)(2,1)} %get-tuple-element.33.rest_2_), channel_id=1, source_target_pairs={{0,4},{1,5},{2,6},{3,7},{4,0},{5,1},{6,2},{7,3}} | collective-permute-start | bytes 3158024 | tf_op jit(solution)/shard_map/ppermute | solution.py:266
  20.0 1.5 copy-start.2
  20.0 51.8 %collective-permute-start.2 = (bf16[4112,128]{1,0:T(8,128)(2,1)}, bf16[4112,128]{1,0:T(8,128)(2,1)S(1)}, u32[]{:S(2)}, u32[]{:S(2)}) collective-permute-start(bf16[4112,128]{1,0:T(8,128)(2,1)} %get-tuple-element.33.rest_2_), channel_id=1, source_target_pairs={{0,2},{1,3},{2,0},{3,1},{4,6},{5,7},{6,4},{7,5}} | collective-permute-start | bytes 3158024 | tf_op jit(solution)/shard_map/ppermute | solution.py:266
  71.8 3.9 %copy-start.1 = (bf16[4112,128]{1,0:T(8,128)(2,1)}, bf16[4112,128]{1,0:T(8,128)(2,1)S(1)}, u32[]{:S(2)}) copy-start(bf16[4112,128]{1,0:T(8,128)(2,1)S(1)} %collective-permute-done.2.rest_2_) | copy-start | bytes 3158020
  73.8 76.1 %collective-permute-start.6 = (bf16[4112,128]{1,0:T(8,128)(2,1)}, bf16[4112,128]{1,0:T(8,128)(2,1)S(1)}, u32[]{:S(2)}, u32[]{:S(2)}) collective-permute-start(bf16[4112,128]{1,0:T(8,128)(2,1)} %get-tuple-element.33.rest_2_), channel_id=1, source_target_pairs={{0,6},{1,7},{2,4},{3,5},{4,2},{5,3},{6,0},{7,1}} | collective-permute-start | bytes 3158024 | tf_op jit(solution)/shard_map/ppermute | solution.py:266
  73.8 76.1 %collective-permute-start.7 = (bf16[4112,128]{1,0:T(8,128)(2,1)}, bf16[4112,128]{1,0:T(8,128)(2,1)S(1)}, u32[]{:S(2)}, u32[]{:S(2)}) collective-permute-start(bf16[4112,128]{1,0:T(8,128)(2,1)} %get-tuple-element.34), channel_id=1, source_target_pairs={{0,7},{1,6},{2,5},{3,4},{4,3},{5,2},{6,1},{7,0}} | collective-permute-start | bytes 3158024 | tf_op jit(solution)/shard_map/ppermute | solution.py:266
  149.9 1.0 copy-start.3
  150.0 1.4 copy-start.4
  187.3 6.8 %collective-permute-start.8 = (bf16[4,6,512,128]{3,2,1,0:T(8,128)(2,1)}, bf16[4,6,512,128]{3,2,1,0:T(8,128)(2,1)S(1)}, u32[]{:S(2)}, u32[]{:S(2)}) collective-permute-start(bf16[4,6,512,128]{3,2,1,0:T(8,128)(2,1)} %get-tuple-element.40), channel_id=1, source_target_pairs={{0,1},{1,0},{2,3},{3,2},{4,5},{5,4},{6,7},{7,6}} | collective-permute-start | bytes 9437192 | tf_op jit(solution)/shard_map/ppermute | solution.py:266

commit v4 on v3

--- a/solution.py
+++ b/solution.py
@@ -61,7 +61,7 @@
             lo, lo_last = cnt_ref[sp * DOCS + d_first], cnt_ref[sp * DOCS + d_last]
             diag = k_piece == q_piece
             hi = jnp.where(diag, off + TILE, piece)
-            need = jnp.where(jnp.logical_and(k_piece <= q_piece, lo < hi), hi - (lo // 128) * 128, 0)
+            need = jnp.where(jnp.logical_and(k_piece <= q_piece, lo < hi), hi - lo, 0)
             blocks = (need + BLOCK - 1) // BLOCK
             start0 = jnp.maximum(hi - BLOCK * blocks, 0)
 

time: 201 us -> 201 us (level)
  no operation moved by 1% of the time
where the time goes in v4:
time: 201 us; the launch traced here: 200 us
  Pallas kernels  160 us (80%)
  local copies, waits for them, and re-layouts  22.4 us (11%)
  starting transfers between devices  7.25 us (4%)
  waiting for transfers between devices  5.52 us (3%)
  other arithmetic  4.88 us (2%)
    pallas_call x3, Pallas kernels, attend(): pl.pallas_call(functools.partial(attend_kernel, masks, group, first, last...  160 us
    ppermute x9, starting transfers between devices, swap(): return lax.ppermute(array, ('cy', 'cx'), pairs)  7.25 us
    ppermute x9, waiting for transfers between devices, swap(): return lax.ppermute(array, ('cy', 'cx'), pairs)  5.52 us
  transfers between devices with their start and end apart: 9, of which 1 were waited for; matrix products, arithmetic and copies ran while one was open for 6% of the time, Pallas kernels for 62%

profile of v4, /device:TPU:6, one launch (start us, length us, event | category | flops | bytes accessed | tf_op | source)
XLA Modules:
  0.0 200.0 jit_solution(4463573555767519224)
XLA Ops:
  0.0 3.2 %constant_dynamic-slice_fusion = (bf16[2048,1,6,128]{3,0,2,1:T(8,128)(2,1)S(1)}, bf16[2048,1,6,128]{3,0,2,1:T(8,128)(2,1)S(1)}) fusion(bf16[2048,2,6,128]{3,0,2,1:T(8,128)(2,1)} %bitcast.46, s32[]{:T(128)S(6)} %select_n.64, s32[]{:T(128)S(6)} %select_n.63), kind=kLoop, calls=%fused_computation.39 | loop fusion | bytes 12582920 | tf_op jit(solution)/shard_map/jit(dynamic_index_in_dim)/dynamic_slice | solution.py:288
  3.3 1.8 copy.22
  5.1 0.2 fusion
  5.3 0.1 copy.15
  5.4 0.1 reshape.152
  5.5 2.4 %copy.24 = bf16[2048,2,128]{2,0,1:T(8,128)(2,1)} copy(bf16[2048,2,128]{2,1,0:T(2,128)(2,1)} %param.5) | data formatting | bytes 2097152 | tf_op args[1]
  7.9 3.7 %copy.14 = bf16[16,128,2,128]{1,3,0,2:T(8,128)(2,1)} copy(bf16[16,128,2,128]{3,2,1,0:T(2,128)(2,1)} %bitcast.52) | data formatting | bytes 2097152 | tf_op jit(solution)/shard_map/reshape | solution.py:283
  11.6 1.7 pad_maximum_fusion
  13.2 1.6 dynamic-slice_bitcast_fusion.1
  14.8 0.4 collective-permute-start
  15.2 0.2 collective-permute-start.5
  15.4 0.0 collective-permute-start.3
  15.5 2.0 %collective-permute-start.4 = (bf16[4112,128]{1,0:T(8,128)(2,1)}, bf16[4112,128]{1,0:T(8,128)(2,1)}, u32[]{:S(2)}, u32[]{:S(2)}) collective-permute-start(bf16[4112,128]{1,0:T(8,128)(2,1)} %get-tuple-element.33.rest_2_), channel_id=1, source_target_pairs={{0,4},{1,5},{2,6},{3,7},{4,0},{5,1},{6,2},{7,3}} | collective-permute-start | bytes 3158024 | tf_op jit(solution)/shard_map/ppermute | solution.py:266
  17.5 1.9 copy.23
  19.3 0.7 slice_bitcast_fusion.1
  20.0 1.5 collective-permute-start.2
  21.6 0.6 convert_element_type.41.cq_ref.cnt_ref
  22.1 49.6 %shard_map.46 = (f32[8,6,16,512]{3,2,1,0:T(8,128)}, f32[8,6,128,512]{3,2,1,0:T(8,128)}) custom-call(s32[1]{0:T(128)} %bitcast.rank_ref, s32[24]{0:T(128)} %convert_element_type.41.cq_ref.cnt_ref, s32[24]{0:T(128)} %convert_element_type.41.cq_ref.cnt_ref, bf16[4,6,512,128]{3,2,1,0:T(8,128)(2,1)} %bitcast.49, ...), custom_call_target="tpu_custom_call" | custom-call | flops 20000000000 | bytes 20971520 | tf_op jit(solution)/shard_map/pallas_call | solution.py:230
  71.8 0.7 slice_bitcast_fusion.6
  72.5 0.7 slice_bitcast_fusion.4
  73.2 0.6 convert_element_type.44.cnt_ref
  73.8 1.8 collective-permute-start.7
  75.7 74.3 %shard_map.47 = (f32[8,6,16,512]{3,2,1,0:T(8,128)}, f32[8,6,128,512]{3,2,1,0:T(8,128)}) custom-call(s32[1]{0:T(128)} %bitcast.rank_ref, s32[24]{0:T(128)} %convert_element_type.41.cq_ref.cnt_ref, s32[48]{0:T(128)} %convert_element_type.44.cnt_ref, bf16[4,6,512,128]{3,2,1,0:T(8,128)(2,1)} %bitcast.50, ...), custom_call_target="tpu_custom_call", output_to_operand_aliasing={{0}: (9, {}), {1}: (10, {})} | custom-call | flops 40000000000 | bytes 20971520 | tf_op jit(solution)/shard_map/pallas_call | solution.py:230
  150.0 0.7 convert_element_type.47.cnt_ref
  150.8 0.1 copy-done.3
  150.9 0.4 copy-done.4
  151.3 35.9 %shard_map.48 = (bf16[4,6,512,128]{3,2,1,0:T(8,128)(2,1)}, bf16[4,6,512,128]{3,2,1,0:T(8,128)(2,1)}) custom-call(s32[1]{0:T(128)} %bitcast.rank_ref, s32[24]{0:T(128)} %convert_element_type.41.cq_ref.cnt_ref, s32[24]{0:T(128)} %convert_element_type.47.cnt_ref, bf16[4,6,512,128]{3,2,1,0:T(8,128)(2,1)} %bitcast.51, ...), custom_call_target="tpu_custom_call" | custom-call | flops 20000000000 | bytes 20971520 | tf_op jit(solution)/shard_map/pallas_call | solution.py:230
  187.3 1.3 collective-permute-start.8
  188.5 5.5 %collective-permute-done.8 = bf16[4,6,512,128]{3,2,1,0:T(8,128)(2,1)S(1)} collective-permute-done((bf16[4,6,512,128]{3,2,1,0:T(8,128)(2,1)}, bf16[4,6,512,128]{3,2,1,0:T(8,128)(2,1)S(1)}, u32[]{:S(2)}, u32[]{:S(2)}) %collective-permute-start.8) | collective-permute-done | bytes 3145760 | tf_op jit(solution)/shard_map/ppermute | solution.py:266
  194.0 2.3 %select_bitcast_fusion.1 = (bf16[1,4,6,512,128]{4,3,2,1,0:T(8,128)(2,1)S(1)}, bf16[1,4,6,512,128]{4,3,2,1,0:T(8,128)(2,1)S(1)}) fusion(bf16[4,6,512,128]{3,2,1,0:T(8,128)(2,1)} %get-tuple-element.39, bf16[4,6,512,128]{3,2,1,0:T(8,128)(2,1)S(1)} %collective-permute-done.8, pred[]{:T(512)S(6)} %eq.7), kind=kLoop, calls=%fused_computation.4 | loop fusion | flops 3145728 | bytes 12582913 | tf_op jit(solution)/shard_map/stack | solution.py:320
  196.3 0.6 maximum_bitcast_fusion
  196.9 3.1 %copy.18 = bf16[4,512,2,6,128]{4,1,0,3,2:T(8,128)(2,1)} copy(bf16[4,512,2,6,128]{4,1,3,0,2:T(8,128)(2,1)S(1)} %maximum_bitcast_fusion) | data formatting | bytes 12582912 | tf_op jit(solution)/shard_map/transpose | solution.py:321
  (31 shorter events, 0.2 us)
Async XLA Ops:
  3.3 1.9 copy-start
  5.1 17.0 %collective-permute-start.1 = (bf16[4,6,512,128]{3,2,1,0:T(8,128)(2,1)}, bf16[4,6,512,128]{3,2,1,0:T(8,128)(2,1)}, u32[]{:S(2)}, u32[]{:S(2)}) collective-permute-start(bf16[4,6,512,128]{3,2,1,0:T(8,128)(2,1)} %bitcast.41), channel_id=1, source_target_pairs={{0,1},{1,0},{2,3},{3,2},{4,5},{5,4},{6,7},{7,6}} | collective-permute-start | bytes 9437192 | tf_op jit(solution)/shard_map/ppermute | solution.py:266
  14.8 5.2 %collective-permute-start = (bf16[4112,128]{1,0:T(8,128)(2,1)}, bf16[4112,128]{1,0:T(8,128)(2,1)S(1)}, u32[]{:S(2)}, u32[]{:S(2)}) collective-permute-start(bf16[4112,128]{1,0:T(8,128)(2,1)} %get-tuple-element.34), channel_id=1, source_target_pairs={{0,1},{1,0},{2,3},{3,2},{4,5},{5,4},{6,7},{7,6}} | collective-permute-start | bytes 3158024 | tf_op jit(solution)/shard_map/ppermute | solution.py:266
  15.2 56.6 %collective-permute-start.5 = (bf16[4112,128]{1,0:T(8,128)(2,1)}, bf16[4112,128]{1,0:T(8,128)(2,1)}, u32[]{:S(2)}, u32[]{:S(2)}) collective-permute-start(bf16[4112,128]{1,0:T(8,128)(2,1)} %get-tuple-element.34), channel_id=1, source_target_pairs={{0,5},{1,4},{2,7},{3,6},{4,1},{5,0},{6,3},{7,2}} | collective-permute-start | bytes 3158024 | tf_op jit(solution)/shard_map/ppermute | solution.py:266
  15.4 56.3 %collective-permute-start.3 = (bf16[4112,128]{1,0:T(8,128)(2,1)}, bf16[4112,128]{1,0:T(8,128)(2,1)}, u32[]{:S(2)}, u32[]{:S(2)}) collective-permute-start(bf16[4112,128]{1,0:T(8,128)(2,1)} %get-tuple-element.34), channel_id=1, source_target_pairs={{0,3},{1,2},{2,1},{3,0},{4,7},{5,6},{6,5},{7,4}} | collective-permute-start | bytes 3158024 | tf_op jit(solution)/shard_map/ppermute | solution.py:266
  15.5 56.3 %collective-permute-start.4 = (bf16[4112,128]{1,0:T(8,128)(2,1)}, bf16[4112,128]{1,0:T(8,128)(2,1)}, u32[]{:S(2)}, u32[]{:S(2)}) collective-permute-start(bf16[4112,128]{1,0:T(8,128)(2,1)} %get-tuple-element.33.rest_2_), channel_id=1, source_target_pairs={{0,4},{1,5},{2,6},{3,7},{4,0},{5,1},{6,2},{7,3}} | collective-permute-start | bytes 3158024 | tf_op jit(solution)/shard_map/ppermute | solution.py:266
  20.0 1.5 copy-start.2
  20.0 51.8 %collective-permute-start.2 = (bf16[4112,128]{1,0:T(8,128)(2,1)}, bf16[4112,128]{1,0:T(8,128)(2,1)S(1)}, u32[]{:S(2)}, u32[]{:S(2)}) collective-permute-start(bf16[4112,128]{1,0:T(8,128)(2,1)} %get-tuple-element.33.rest_2_), channel_id=1, source_target_pairs={{0,2},{1,3},{2,0},{3,1},{4,6},{5,7},{6,4},{7,5}} | collective-permute-start | bytes 3158024 | tf_op jit(solution)/shard_map/ppermute | solution.py:266
  71.8 3.9 %copy-start.1 = (bf16[4112,128]{1,0:T(8,128)(2,1)}, bf16[4112,128]{1,0:T(8,128)(2,1)S(1)}, u32[]{:S(2)}) copy-start(bf16[4112,128]{1,0:T(8,128)(2,1)S(1)} %collective-permute-done.2.rest_2_) | copy-start | bytes 3158020
  73.8 76.1 %collective-permute-start.6 = (bf16[4112,128]{1,0:T(8,128)(2,1)}, bf16[4112,128]{1,0:T(8,128)(2,1)S(1)}, u32[]{:S(2)}, u32[]{:S(2)}) collective-permute-start(bf16[4112,128]{1,0:T(8,128)(2,1)} %get-tuple-element.33.rest_2_), channel_id=1, source_target_pairs={{0,6},{1,7},{2,4},{3,5},{4,2},{5,3},{6,0},{7,1}} | collective-permute-start | bytes 3158024 | tf_op jit(solution)/shard_map/ppermute | solution.py:266
  73.8 76.1 %collective-permute-start.7 = (bf16[4112,128]{1,0:T(8,128)(2,1)}, bf16[4112,128]{1,0:T(8,128)(2,1)S(1)}, u32[]{:S(2)}, u32[]{:S(2)}) collective-permute-start(bf16[4112,128]{1,0:T(8,128)(2,1)} %get-tuple-element.34), channel_id=1, source_target_pairs={{0,7},{1,6},{2,5},{3,4},{4,3},{5,2},{6,1},{7,0}} | collective-permute-start | bytes 3158024 | tf_op jit(solution)/shard_map/ppermute | solution.py:266
  149.9 1.0 copy-start.3
  150.0 1.4 copy-start.4
  187.3 6.8 %collective-permute-start.8 = (bf16[4,6,512,128]{3,2,1,0:T(8,128)(2,1)}, bf16[4,6,512,128]{3,2,1,0:T(8,128)(2,1)S(1)}, u32[]{:S(2)}, u32[]{:S(2)}) collective-permute-start(bf16[4,6,512,128]{3,2,1,0:T(8,128)(2,1)} %get-tuple-element.40), channel_id=1, source_target_pairs={{0,1},{1,0},{2,3},{3,2},{4,5},{5,4},{6,7},{7,6}} | collective-permute-start | bytes 9437192 | tf_op jit(solution)/shard_map/ppermute | solution.py:266
